TPU v7x, 32 devices: a whole 2x2x4 slice. The times are simulated.
32 devices in a mesh: row: 4 (over z), col: 8 (over y, x, core).
Axes of the slice: x: 2, y: 2, z: 4, core: 2. Of those that a mesh axis runs over, the one named last changes fastest.
Arguments:
- point_coords: float32 [1024, 3, 256], P(('row', 'col')), may hold values from 0 to 10
- fluid_force: float32 [1024, 3, 256], P(('row', 'col')), may hold values from -6 to 6
- tile_clusters: int32 [1024, 8], P(('row', 'col')), may hold values from 0 to 511, as said below
- pu_level: int32 [1024, 8, 256], P(('row', 'col')), may hold values from 0 to 15
- node_coords: float32 [512, 3, 512], P(('row', 'col')), may hold values from 0 to 10
- node_disp: float32 [512, 3, 512], P(('row', 'col')), may hold values from -6 to 6
- inverse: float32 [512, 512, 512], P(('row', 'col')), may hold values from -0.25 to 0.25
Outputs:
- point_disp: float32 [1024, 3, 256], P(('row', 'col'))
- node_force: float32 [512, 3, 512], P(('row', 'col'))
Inputs may be any that keep to these rules, and one draw needn't show every extreme that they name: `tile_clusters`: cluster c lives with rows c of the cluster arrays; tile t's k-th entry names a cluster intersecting it, possibly more than once in a tile. Among the 256 entries of one device's tiles, at most 8 name clusters of any one device (clusters d * 16 to d * 16 + 15).
All inputs are finite; a program needn't handle non-finite values.
Results may differ from a plain program's by a relative error of at most 0.0003.
Values sent between devices are 32-bit elements; how exact they have to be, the bound alone decides.
No kernel may reach another device: no remote copies, remote signals or barrier semaphores. Data moves between devices by JAX's collectives and lax.ppermute only.
A program may use at most 128 MiB of HBM per device.

v0:
```python
import math

import jax
import jax.numpy as jnp
from jax import lax
from jax.sharding import PartitionSpec as P

CAP = 8


def kernel(points, node_rows):
    offset = points[..., :, :, None] - node_rows[..., :, None, :]
    scaled = jnp.sqrt(jnp.sum(offset * offset, axis=-3))
    return jnp.maximum(1.0 - scaled, 0.0) ** 4 * (4.0 * scaled + 1.0)


def on_device(point_coords, fluid_force, tile_clusters, pu_level, node_coords, node_disp, inverse):
    highest = lax.Precision.HIGHEST
    devices = lax.axis_size(("row", "col"))
    slot_total = devices * CAP
    tile_total, kslots = tile_clusters.shape
    pair_total = tile_total * kslots
    node_count = node_coords.shape[2]
    tile_width = point_coords.shape[2]
    local_count = node_coords.shape[0]
    coeffs = jnp.einsum("cin,cnm->cim", node_disp, inverse, precision=highest)
    levels = pu_level.astype(jnp.float32) + 1.0
    weights = levels / jnp.sum(levels, axis=1, keepdims=True)
    cluster_ids = tile_clusters.reshape(-1)
    owner_dev = cluster_ids // local_count
    local_id = cluster_ids % local_count
    owner_hits = (owner_dev[:, None] == jnp.arange(devices, dtype=jnp.int32)[None, :]).astype(
        jnp.int32
    )
    earlier = jnp.cumsum(owner_hits, axis=0) - owner_hits
    slot_of = owner_dev * CAP + jnp.sum(earlier * owner_hits, axis=1)
    slot_hits = slot_of[:, None] == jnp.arange(slot_total, dtype=jnp.int32)[None, :]
    wanted = jnp.sum(jnp.where(slot_hits, local_id[:, None] + 1, 0), axis=0) - 1
    loads = weights[:, :, None, :] * fluid_force[:, None, :, :]
    point_rows = jnp.broadcast_to(point_coords[:, None], loads.shape)
    packed = jnp.concatenate((point_rows, loads), axis=2).reshape(pair_total, 6, tile_width)
    outgoing = jnp.zeros((slot_total, 6, tile_width), jnp.float32).at[slot_of].set(packed)
    asked_ids, arrived = (
        lax.all_to_all(
            wanted.reshape(devices, CAP), ("row", "col"), split_axis=0, concat_axis=0, tiled=True
        ),
        lax.all_to_all(
            outgoing.reshape(devices, CAP, 6, tile_width),
            ("row", "col"),
            split_axis=0,
            concat_axis=0,
            tiled=True,
        ),
    )
    asked_ids = asked_ids.reshape(slot_total)
    arrived = arrived.reshape(slot_total, 6, tile_width)
    group_size = math.gcd(slot_total, 8)

    def per_group(bundle):
        slot_ids, slot_rows = bundle
        kernel_vals = kernel(slot_rows[:, :3], jnp.take(node_coords, slot_ids, axis=0))
        values = jnp.einsum(
            "bpn,bin->bip", kernel_vals, jnp.take(coeffs, slot_ids, axis=0), precision=highest
        )
        partial_value = jnp.einsum("bpn,bip->bin", kernel_vals, slot_rows[:, 3:], precision=highest)
        return (values, partial_value)

    slot_ids = jnp.maximum(asked_ids, 0).reshape(-1, group_size)
    values, partial_value = lax.map(
        per_group, (slot_ids, arrived.reshape(-1, group_size, 6, tile_width))
    )
    chosen = (asked_ids[:, None] == jnp.arange(local_count, dtype=jnp.int32)[None, :]).astype(
        jnp.float32
    )
    node_force = jnp.einsum(
        "sc,sin->cin", chosen, partial_value.reshape(slot_total, 3, node_count), precision=highest
    )
    returned = lax.all_to_all(
        values, ("row", "col"), split_axis=0, concat_axis=0, tiled=True
    ).reshape(slot_total, 3, tile_width)
    own_rows = jnp.take(returned, slot_of, axis=0).reshape(tile_total, kslots, 3, tile_width)
    point_disp = jnp.sum(weights[:, :, None, :] * own_rows, axis=1)
    return (point_disp, node_force)


def solution(mesh):
    placed = (
        P(("row", "col"), None, None),
        P(("row", "col"), None, None),
        P(("row", "col"), None),
        P(("row", "col"), None, None),
        P(("row", "col"), None, None),
        P(("row", "col"), None, None),
        P(("row", "col"), None, None),
    )
    return jax.shard_map(
        on_device,
        mesh=mesh,
        in_specs=placed,
        out_specs=(P(("row", "col"), None, None), P(("row", "col"), None, None)),
        check_vma=False,
    )
```

profile of v0, /device:TPU:0, one launch (start us, length us, event | category | flops | bytes accessed | tf_op | source)
XLA Modules:
  0.0 681.9 jit_solution(13986326841388052322)
XLA Ops:
  3.4 7.3 %all-to-all-start = ((s32[32,1,8]{2,1,0:T(1,128)}), s32[32,1,8]{2,1,0:T(1,128)S(1)}, u32[]{:S(2)}, u32[]{:S(2)}) async-start(s32[32,1,8]{2,1,0:T(1,128)} %bitcast.5), calls=%async_computation | async-start | bytes 32768 | tf_op jit(solution)/shard_map/all_to_all | solution.py:44
  16.2 18.6 %scatter_fusion = f32[256,6,256]{2,1,0:T(8,128)S(1)} fusion(f32[256,6,256]{2,1,0:T(8,128)S(1)} %broadcast_in_dim.72, s32[256]{0:T(256)S(1)} %bitcast.67, f32[256,6,256]{2,1,0:T(8,128)} %pad_maximum_fusion), kind=kCustom, calls=%fused_computation.3 | custom fusion | bytes 4719616 | tf_op jit(solution)/shard_map/scatter | solution.py:42
  36.7 5.8 all-to-all-start.1
  42.7 11.5 %fusion.27 = f32[16,3,512]{2,1,0:T(4,128)S(1)} fusion(f32[16,512,512]{2,1,0:T(8,128)} %param.17, f32[16,3,512]{2,0,1:T(8,128)S(1)} %copy-done.1), kind=kOutput, calls=%fused_computation.48 | convolution fusion | flops 150994944 | bytes 16973824 | tf_op jit(solution)/shard_map/cin,cnm->cim/dot_general | solution.py:26
  55.4 24.8 %all-to-all-done.1 = f32[32,8,6,256]{3,1,2,0:T(8,128)S(1)} async-done(((f32[32,8,6,256]{3,1,2,0:T(8,128)}), f32[32,8,6,256]{3,1,2,0:T(8,128)S(1)}, u32[]{:S(2)}, u32[]{:S(2)}) %all-to-all-start.1) | async-done | bytes 1572896 | tf_op jit(solution)/shard_map/all_to_all | solution.py:47
  80.2 574.3 %while.12 = (s32[]{:T(128)}, f32[32,8,3,256]{3,1,2,0:T(8,128)}, f32[32,8,3,512]{3,2,1,0:T(4,128)}, s32[32,8]{1,0:T(8,128)S(1)}, f32[16,3,512]{2,1,0:T(4,128)S(1)...) while((s32[]{:T(128)}, f32[32,8,3,256]{3,1,2,0:T(8,128)}, ...), condition=%wide.region_8.10_spmd, body=%wide.region_6.9_spmd.sunk | while | flops 98591792 | bytes 30200128 | solution.py:69
  85.5 7.4 %fusion.56 = f32[1,8,3,256]{3,2,1,0:T(4,128)S(1)} fusion(f32[8,256,512]{2,1,0:T(8,128)} %multiply_reduce_fusion.3, f32[8,3,512]{2,1,0:T(4,128)S(1)} %gather_fusion.1, pred[8]{0:T(512)(128)(4,1)S(1)} %get-tuple-element.152), kind=kOutput, calls=%fused_computation.16.clone.1 | convolution fusion | flops 45101056 | bytes 4268040 | tf_op jit(solution)/shard_map/while/body/eval_jaxpr/bpn,bin->bip/dot_general | solution.py:62
  93.6 4.6 fusion.57
  103.5 7.4 %fusion.56 = f32[1,8,3,256]{3,2,1,0:T(4,128)S(1)} fusion(f32[8,256,512]{2,1,0:T(8,128)} %multiply_reduce_fusion.3, f32[8,3,512]{2,1,0:T(4,128)S(1)} %gather_fusion.1, pred[8]{0:T(512)(128)(4,1)S(1)} %get-tuple-element.152), kind=kOutput, calls=%fused_computation.16.clone.1 | convolution fusion | flops 45101056 | bytes 4268040 | tf_op jit(solution)/shard_map/while/body/eval_jaxpr/bpn,bin->bip/dot_general | solution.py:62
  121.4 7.4 %fusion.56 = f32[1,8,3,256]{3,2,1,0:T(4,128)S(1)} fusion(f32[8,256,512]{2,1,0:T(8,128)} %multiply_reduce_fusion.3, f32[8,3,512]{2,1,0:T(4,128)S(1)} %gather_fusion.1, pred[8]{0:T(512)(128)(4,1)S(1)} %get-tuple-element.152), kind=kOutput, calls=%fused_computation.16.clone.1 | convolution fusion | flops 45101056 | bytes 4268040 | tf_op jit(solution)/shard_map/while/body/eval_jaxpr/bpn,bin->bip/dot_general | solution.py:62
  139.4 7.4 %fusion.56 = f32[1,8,3,256]{3,2,1,0:T(4,128)S(1)} fusion(f32[8,256,512]{2,1,0:T(8,128)} %multiply_reduce_fusion.3, f32[8,3,512]{2,1,0:T(4,128)S(1)} %gather_fusion.1, pred[8]{0:T(512)(128)(4,1)S(1)} %get-tuple-element.152), kind=kOutput, calls=%fused_computation.16.clone.1 | convolution fusion | flops 45101056 | bytes 4268040 | tf_op jit(solution)/shard_map/while/body/eval_jaxpr/bpn,bin->bip/dot_general | solution.py:62
  157.3 7.4 %fusion.56 = f32[1,8,3,256]{3,2,1,0:T(4,128)S(1)} fusion(f32[8,256,512]{2,1,0:T(8,128)} %multiply_reduce_fusion.3, f32[8,3,512]{2,1,0:T(4,128)S(1)} %gather_fusion.1, pred[8]{0:T(512)(128)(4,1)S(1)} %get-tuple-element.152), kind=kOutput, calls=%fused_computation.16.clone.1 | convolution fusion | flops 45101056 | bytes 4268040 | tf_op jit(solution)/shard_map/while/body/eval_jaxpr/bpn,bin->bip/dot_general | solution.py:62
  175.3 7.4 %fusion.56 = f32[1,8,3,256]{3,2,1,0:T(4,128)S(1)} fusion(f32[8,256,512]{2,1,0:T(8,128)} %multiply_reduce_fusion.3, f32[8,3,512]{2,1,0:T(4,128)S(1)} %gather_fusion.1, pred[8]{0:T(512)(128)(4,1)S(1)} %get-tuple-element.152), kind=kOutput, calls=%fused_computation.16.clone.1 | convolution fusion | flops 45101056 | bytes 4268040 | tf_op jit(solution)/shard_map/while/body/eval_jaxpr/bpn,bin->bip/dot_general | solution.py:62
  183.3 4.5 fusion.57
  193.2 7.4 %fusion.56 = f32[1,8,3,256]{3,2,1,0:T(4,128)S(1)} fusion(f32[8,256,512]{2,1,0:T(8,128)} %multiply_reduce_fusion.3, f32[8,3,512]{2,1,0:T(4,128)S(1)} %gather_fusion.1, pred[8]{0:T(512)(128)(4,1)S(1)} %get-tuple-element.152), kind=kOutput, calls=%fused_computation.16.clone.1 | convolution fusion | flops 45101056 | bytes 4268040 | tf_op jit(solution)/shard_map/while/body/eval_jaxpr/bpn,bin->bip/dot_general | solution.py:62
  201.3 4.5 fusion.57
  211.2 7.4 %fusion.56 = f32[1,8,3,256]{3,2,1,0:T(4,128)S(1)} fusion(f32[8,256,512]{2,1,0:T(8,128)} %multiply_reduce_fusion.3, f32[8,3,512]{2,1,0:T(4,128)S(1)} %gather_fusion.1, pred[8]{0:T(512)(128)(4,1)S(1)} %get-tuple-element.152), kind=kOutput, calls=%fused_computation.16.clone.1 | convolution fusion | flops 45101056 | bytes 4268040 | tf_op jit(solution)/shard_map/while/body/eval_jaxpr/bpn,bin->bip/dot_general | solution.py:62
  229.1 7.4 %fusion.56 = f32[1,8,3,256]{3,2,1,0:T(4,128)S(1)} fusion(f32[8,256,512]{2,1,0:T(8,128)} %multiply_reduce_fusion.3, f32[8,3,512]{2,1,0:T(4,128)S(1)} %gather_fusion.1, pred[8]{0:T(512)(128)(4,1)S(1)} %get-tuple-element.152), kind=kOutput, calls=%fused_computation.16.clone.1 | convolution fusion | flops 45101056 | bytes 4268040 | tf_op jit(solution)/shard_map/while/body/eval_jaxpr/bpn,bin->bip/dot_general | solution.py:62
  247.1 7.4 %fusion.56 = f32[1,8,3,256]{3,2,1,0:T(4,128)S(1)} fusion(f32[8,256,512]{2,1,0:T(8,128)} %multiply_reduce_fusion.3, f32[8,3,512]{2,1,0:T(4,128)S(1)} %gather_fusion.1, pred[8]{0:T(512)(128)(4,1)S(1)} %get-tuple-element.152), kind=kOutput, calls=%fused_computation.16.clone.1 | convolution fusion | flops 45101056 | bytes 4268040 | tf_op jit(solution)/shard_map/while/body/eval_jaxpr/bpn,bin->bip/dot_general | solution.py:62
  265.0 7.4 %fusion.56 = f32[1,8,3,256]{3,2,1,0:T(4,128)S(1)} fusion(f32[8,256,512]{2,1,0:T(8,128)} %multiply_reduce_fusion.3, f32[8,3,512]{2,1,0:T(4,128)S(1)} %gather_fusion.1, pred[8]{0:T(512)(128)(4,1)S(1)} %get-tuple-element.152), kind=kOutput, calls=%fused_computation.16.clone.1 | convolution fusion | flops 45101056 | bytes 4268040 | tf_op jit(solution)/shard_map/while/body/eval_jaxpr/bpn,bin->bip/dot_general | solution.py:62
  283.0 7.4 %fusion.56 = f32[1,8,3,256]{3,2,1,0:T(4,128)S(1)} fusion(f32[8,256,512]{2,1,0:T(8,128)} %multiply_reduce_fusion.3, f32[8,3,512]{2,1,0:T(4,128)S(1)} %gather_fusion.1, pred[8]{0:T(512)(128)(4,1)S(1)} %get-tuple-element.152), kind=kOutput, calls=%fused_computation.16.clone.1 | convolution fusion | flops 45101056 | bytes 4268040 | tf_op jit(solution)/shard_map/while/body/eval_jaxpr/bpn,bin->bip/dot_general | solution.py:62
  300.9 7.4 %fusion.56 = f32[1,8,3,256]{3,2,1,0:T(4,128)S(1)} fusion(f32[8,256,512]{2,1,0:T(8,128)} %multiply_reduce_fusion.3, f32[8,3,512]{2,1,0:T(4,128)S(1)} %gather_fusion.1, pred[8]{0:T(512)(128)(4,1)S(1)} %get-tuple-element.152), kind=kOutput, calls=%fused_computation.16.clone.1 | convolution fusion | flops 45101056 | bytes 4268040 | tf_op jit(solution)/shard_map/while/body/eval_jaxpr/bpn,bin->bip/dot_general | solution.py:62
  318.8 7.4 %fusion.56 = f32[1,8,3,256]{3,2,1,0:T(4,128)S(1)} fusion(f32[8,256,512]{2,1,0:T(8,128)} %multiply_reduce_fusion.3, f32[8,3,512]{2,1,0:T(4,128)S(1)} %gather_fusion.1, pred[8]{0:T(512)(128)(4,1)S(1)} %get-tuple-element.152), kind=kOutput, calls=%fused_computation.16.clone.1 | convolution fusion | flops 45101056 | bytes 4268040 | tf_op jit(solution)/shard_map/while/body/eval_jaxpr/bpn,bin->bip/dot_general | solution.py:62
  336.8 7.4 %fusion.56 = f32[1,8,3,256]{3,2,1,0:T(4,128)S(1)} fusion(f32[8,256,512]{2,1,0:T(8,128)} %multiply_reduce_fusion.3, f32[8,3,512]{2,1,0:T(4,128)S(1)} %gather_fusion.1, pred[8]{0:T(512)(128)(4,1)S(1)} %get-tuple-element.152), kind=kOutput, calls=%fused_computation.16.clone.1 | convolution fusion | flops 45101056 | bytes 4268040 | tf_op jit(solution)/shard_map/while/body/eval_jaxpr/bpn,bin->bip/dot_general | solution.py:62
  354.7 7.4 %fusion.56 = f32[1,8,3,256]{3,2,1,0:T(4,128)S(1)} fusion(f32[8,256,512]{2,1,0:T(8,128)} %multiply_reduce_fusion.3, f32[8,3,512]{2,1,0:T(4,128)S(1)} %gather_fusion.1, pred[8]{0:T(512)(128)(4,1)S(1)} %get-tuple-element.152), kind=kOutput, calls=%fused_computation.16.clone.1 | convolution fusion | flops 45101056 | bytes 4268040 | tf_op jit(solution)/shard_map/while/body/eval_jaxpr/bpn,bin->bip/dot_general | solution.py:62
  372.7 7.4 %fusion.56 = f32[1,8,3,256]{3,2,1,0:T(4,128)S(1)} fusion(f32[8,256,512]{2,1,0:T(8,128)} %multiply_reduce_fusion.3, f32[8,3,512]{2,1,0:T(4,128)S(1)} %gather_fusion.1, pred[8]{0:T(512)(128)(4,1)S(1)} %get-tuple-element.152), kind=kOutput, calls=%fused_computation.16.clone.1 | convolution fusion | flops 45101056 | bytes 4268040 | tf_op jit(solution)/shard_map/while/body/eval_jaxpr/bpn,bin->bip/dot_general | solution.py:62
  380.7 4.5 fusion.57
  390.6 7.4 %fusion.56 = f32[1,8,3,256]{3,2,1,0:T(4,128)S(1)} fusion(f32[8,256,512]{2,1,0:T(8,128)} %multiply_reduce_fusion.3, f32[8,3,512]{2,1,0:T(4,128)S(1)} %gather_fusion.1, pred[8]{0:T(512)(128)(4,1)S(1)} %get-tuple-element.152), kind=kOutput, calls=%fused_computation.16.clone.1 | convolution fusion | flops 45101056 | bytes 4268040 | tf_op jit(solution)/shard_map/while/body/eval_jaxpr/bpn,bin->bip/dot_general | solution.py:62
  408.5 7.4 %fusion.56 = f32[1,8,3,256]{3,2,1,0:T(4,128)S(1)} fusion(f32[8,256,512]{2,1,0:T(8,128)} %multiply_reduce_fusion.3, f32[8,3,512]{2,1,0:T(4,128)S(1)} %gather_fusion.1, pred[8]{0:T(512)(128)(4,1)S(1)} %get-tuple-element.152), kind=kOutput, calls=%fused_computation.16.clone.1 | convolution fusion | flops 45101056 | bytes 4268040 | tf_op jit(solution)/shard_map/while/body/eval_jaxpr/bpn,bin->bip/dot_general | solution.py:62
  426.5 7.4 %fusion.56 = f32[1,8,3,256]{3,2,1,0:T(4,128)S(1)} fusion(f32[8,256,512]{2,1,0:T(8,128)} %multiply_reduce_fusion.3, f32[8,3,512]{2,1,0:T(4,128)S(1)} %gather_fusion.1, pred[8]{0:T(512)(128)(4,1)S(1)} %get-tuple-element.152), kind=kOutput, calls=%fused_computation.16.clone.1 | convolution fusion | flops 45101056 | bytes 4268040 | tf_op jit(solution)/shard_map/while/body/eval_jaxpr/bpn,bin->bip/dot_general | solution.py:62
  444.4 7.4 %fusion.56 = f32[1,8,3,256]{3,2,1,0:T(4,128)S(1)} fusion(f32[8,256,512]{2,1,0:T(8,128)} %multiply_reduce_fusion.3, f32[8,3,512]{2,1,0:T(4,128)S(1)} %gather_fusion.1, pred[8]{0:T(512)(128)(4,1)S(1)} %get-tuple-element.152), kind=kOutput, calls=%fused_computation.16.clone.1 | convolution fusion | flops 45101056 | bytes 4268040 | tf_op jit(solution)/shard_map/while/body/eval_jaxpr/bpn,bin->bip/dot_general | solution.py:62
  452.5 4.5 fusion.57
  462.4 7.4 %fusion.56 = f32[1,8,3,256]{3,2,1,0:T(4,128)S(1)} fusion(f32[8,256,512]{2,1,0:T(8,128)} %multiply_reduce_fusion.3, f32[8,3,512]{2,1,0:T(4,128)S(1)} %gather_fusion.1, pred[8]{0:T(512)(128)(4,1)S(1)} %get-tuple-element.152), kind=kOutput, calls=%fused_computation.16.clone.1 | convolution fusion | flops 45101056 | bytes 4268040 | tf_op jit(solution)/shard_map/while/body/eval_jaxpr/bpn,bin->bip/dot_general | solution.py:62
  480.3 7.4 %fusion.56 = f32[1,8,3,256]{3,2,1,0:T(4,128)S(1)} fusion(f32[8,256,512]{2,1,0:T(8,128)} %multiply_reduce_fusion.3, f32[8,3,512]{2,1,0:T(4,128)S(1)} %gather_fusion.1, pred[8]{0:T(512)(128)(4,1)S(1)} %get-tuple-element.152), kind=kOutput, calls=%fused_computation.16.clone.1 | convolution fusion | flops 45101056 | bytes 4268040 | tf_op jit(solution)/shard_map/while/body/eval_jaxpr/bpn,bin->bip/dot_general | solution.py:62
  498.3 7.4 %fusion.56 = f32[1,8,3,256]{3,2,1,0:T(4,128)S(1)} fusion(f32[8,256,512]{2,1,0:T(8,128)} %multiply_reduce_fusion.3, f32[8,3,512]{2,1,0:T(4,128)S(1)} %gather_fusion.1, pred[8]{0:T(512)(128)(4,1)S(1)} %get-tuple-element.152), kind=kOutput, calls=%fused_computation.16.clone.1 | convolution fusion | flops 45101056 | bytes 4268040 | tf_op jit(solution)/shard_map/while/body/eval_jaxpr/bpn,bin->bip/dot_general | solution.py:62
  506.3 4.5 fusion.57
  516.2 7.4 %fusion.56 = f32[1,8,3,256]{3,2,1,0:T(4,128)S(1)} fusion(f32[8,256,512]{2,1,0:T(8,128)} %multiply_reduce_fusion.3, f32[8,3,512]{2,1,0:T(4,128)S(1)} %gather_fusion.1, pred[8]{0:T(512)(128)(4,1)S(1)} %get-tuple-element.152), kind=kOutput, calls=%fused_computation.16.clone.1 | convolution fusion | flops 45101056 | bytes 4268040 | tf_op jit(solution)/shard_map/while/body/eval_jaxpr/bpn,bin->bip/dot_general | solution.py:62
  524.3 4.5 fusion.57
  534.2 7.4 %fusion.56 = f32[1,8,3,256]{3,2,1,0:T(4,128)S(1)} fusion(f32[8,256,512]{2,1,0:T(8,128)} %multiply_reduce_fusion.3, f32[8,3,512]{2,1,0:T(4,128)S(1)} %gather_fusion.1, pred[8]{0:T(512)(128)(4,1)S(1)} %get-tuple-element.152), kind=kOutput, calls=%fused_computation.16.clone.1 | convolution fusion | flops 45101056 | bytes 4268040 | tf_op jit(solution)/shard_map/while/body/eval_jaxpr/bpn,bin->bip/dot_general | solution.py:62
  552.1 7.4 %fusion.56 = f32[1,8,3,256]{3,2,1,0:T(4,128)S(1)} fusion(f32[8,256,512]{2,1,0:T(8,128)} %multiply_reduce_fusion.3, f32[8,3,512]{2,1,0:T(4,128)S(1)} %gather_fusion.1, pred[8]{0:T(512)(128)(4,1)S(1)} %get-tuple-element.152), kind=kOutput, calls=%fused_computation.16.clone.1 | convolution fusion | flops 45101056 | bytes 4268040 | tf_op jit(solution)/shard_map/while/body/eval_jaxpr/bpn,bin->bip/dot_general | solution.py:62
  570.1 7.4 %fusion.56 = f32[1,8,3,256]{3,2,1,0:T(4,128)S(1)} fusion(f32[8,256,512]{2,1,0:T(8,128)} %multiply_reduce_fusion.3, f32[8,3,512]{2,1,0:T(4,128)S(1)} %gather_fusion.1, pred[8]{0:T(512)(128)(4,1)S(1)} %get-tuple-element.152), kind=kOutput, calls=%fused_computation.16.clone.1 | convolution fusion | flops 45101056 | bytes 4268040 | tf_op jit(solution)/shard_map/while/body/eval_jaxpr/bpn,bin->bip/dot_general | solution.py:62
  578.1 4.5 fusion.57
  588.0 7.4 %fusion.56 = f32[1,8,3,256]{3,2,1,0:T(4,128)S(1)} fusion(f32[8,256,512]{2,1,0:T(8,128)} %multiply_reduce_fusion.3, f32[8,3,512]{2,1,0:T(4,128)S(1)} %gather_fusion.1, pred[8]{0:T(512)(128)(4,1)S(1)} %get-tuple-element.152), kind=kOutput, calls=%fused_computation.16.clone.1 | convolution fusion | flops 45101056 | bytes 4268040 | tf_op jit(solution)/shard_map/while/body/eval_jaxpr/bpn,bin->bip/dot_general | solution.py:62
  605.9 7.4 %fusion.56 = f32[1,8,3,256]{3,2,1,0:T(4,128)S(1)} fusion(f32[8,256,512]{2,1,0:T(8,128)} %multiply_reduce_fusion.3, f32[8,3,512]{2,1,0:T(4,128)S(1)} %gather_fusion.1, pred[8]{0:T(512)(128)(4,1)S(1)} %get-tuple-element.152), kind=kOutput, calls=%fused_computation.16.clone.1 | convolution fusion | flops 45101056 | bytes 4268040 | tf_op jit(solution)/shard_map/while/body/eval_jaxpr/bpn,bin->bip/dot_general | solution.py:62
  614.0 4.5 fusion.57
  623.9 7.4 %fusion.56 = f32[1,8,3,256]{3,2,1,0:T(4,128)S(1)} fusion(f32[8,256,512]{2,1,0:T(8,128)} %multiply_reduce_fusion.3, f32[8,3,512]{2,1,0:T(4,128)S(1)} %gather_fusion.1, pred[8]{0:T(512)(128)(4,1)S(1)} %get-tuple-element.152), kind=kOutput, calls=%fused_computation.16.clone.1 | convolution fusion | flops 45101056 | bytes 4268040 | tf_op jit(solution)/shard_map/while/body/eval_jaxpr/bpn,bin->bip/dot_general | solution.py:62
  641.8 7.4 %fusion.56 = f32[1,8,3,256]{3,2,1,0:T(4,128)S(1)} fusion(f32[8,256,512]{2,1,0:T(8,128)} %multiply_reduce_fusion.3, f32[8,3,512]{2,1,0:T(4,128)S(1)} %gather_fusion.1, pred[8]{0:T(512)(128)(4,1)S(1)} %get-tuple-element.152), kind=kOutput, calls=%fused_computation.16.clone.1 | convolution fusion | flops 45101056 | bytes 4268040 | tf_op jit(solution)/shard_map/while/body/eval_jaxpr/bpn,bin->bip/dot_general | solution.py:62
  661.9 16.9 %all-to-all-done.2 = f32[32,8,3,256]{3,1,2,0:T(8,128)S(1)} async-done(((f32[32,8,3,256]{3,1,2,0:T(8,128)}), f32[32,8,3,256]{3,1,2,0:T(8,128)S(1)}, u32[]{:S(2)}, u32[]{:S(2)}) %all-to-all-start.2) | async-done | bytes 786464 | tf_op jit(solution)/shard_map/all_to_all | solution.py:78
  (453 shorter events, 316.2 us)
Async XLA Ops:
  3.4 33.3 %all-to-all-start = ((s32[32,1,8]{2,1,0:T(1,128)}), s32[32,1,8]{2,1,0:T(1,128)S(1)}, u32[]{:S(2)}, u32[]{:S(2)}) async-start(s32[32,1,8]{2,1,0:T(1,128)} %bitcast.5), calls=%async_computation | async-start | bytes 32768 | tf_op jit(solution)/shard_map/all_to_all | solution.py:44
  34.8 7.7 %copy-start.2 = (f32[16,3,512]{2,0,1:T(8,128)S(1)}, f32[16,3,512]{2,0,1:T(8,128)}, u32[]{:S(2)}) copy-start(f32[16,3,512]{2,0,1:T(8,128)} %param.15) | copy-start | bytes 294916
  34.9 7.8 %copy-start.1 = (f32[16,3,512]{2,0,1:T(8,128)S(1)}, f32[16,3,512]{2,0,1:T(8,128)}, u32[]{:S(2)}) copy-start(f32[16,3,512]{2,0,1:T(8,128)} %param.16) | copy-start | bytes 294916
  36.7 43.5 %all-to-all-start.1 = ((f32[32,8,6,256]{3,1,2,0:T(8,128)}), f32[32,8,6,256]{3,1,2,0:T(8,128)S(1)}, u32[]{:S(2)}, u32[]{:S(2)}) async-start(f32[32,8,6,256]{3,1,2,0:T(8,128)} %copy.97), calls=%async_computation.1 | async-start | bytes 3145728 | tf_op jit(solution)/shard_map/all_to_all | solution.py:47
  85.5 8.0 %copy-start = (f32[8,256,512]{2,1,0:T(8,128)S(1)}, f32[8,256,512]{2,1,0:T(8,128)}, u32[]{:S(2)}) copy-start(f32[8,256,512]{2,1,0:T(8,128)} %multiply_reduce_fusion.3) | copy-start | bytes 12582916 | tf_op jit(solution)/shard_map/while
  103.5 8.1 %copy-start = (f32[8,256,512]{2,1,0:T(8,128)S(1)}, f32[8,256,512]{2,1,0:T(8,128)}, u32[]{:S(2)}) copy-start(f32[8,256,512]{2,1,0:T(8,128)} %multiply_reduce_fusion.3) | copy-start | bytes 12582916 | tf_op jit(solution)/shard_map/while
  121.4 8.1 %copy-start = (f32[8,256,512]{2,1,0:T(8,128)S(1)}, f32[8,256,512]{2,1,0:T(8,128)}, u32[]{:S(2)}) copy-start(f32[8,256,512]{2,1,0:T(8,128)} %multiply_reduce_fusion.3) | copy-start | bytes 12582916 | tf_op jit(solution)/shard_map/while
  139.4 8.0 %copy-start = (f32[8,256,512]{2,1,0:T(8,128)S(1)}, f32[8,256,512]{2,1,0:T(8,128)}, u32[]{:S(2)}) copy-start(f32[8,256,512]{2,1,0:T(8,128)} %multiply_reduce_fusion.3) | copy-start | bytes 12582916 | tf_op jit(solution)/shard_map/while
  157.3 8.0 %copy-start = (f32[8,256,512]{2,1,0:T(8,128)S(1)}, f32[8,256,512]{2,1,0:T(8,128)}, u32[]{:S(2)}) copy-start(f32[8,256,512]{2,1,0:T(8,128)} %multiply_reduce_fusion.3) | copy-start | bytes 12582916 | tf_op jit(solution)/shard_map/while
  175.3 8.1 %copy-start = (f32[8,256,512]{2,1,0:T(8,128)S(1)}, f32[8,256,512]{2,1,0:T(8,128)}, u32[]{:S(2)}) copy-start(f32[8,256,512]{2,1,0:T(8,128)} %multiply_reduce_fusion.3) | copy-start | bytes 12582916 | tf_op jit(solution)/shard_map/while
  193.2 8.1 %copy-start = (f32[8,256,512]{2,1,0:T(8,128)S(1)}, f32[8,256,512]{2,1,0:T(8,128)}, u32[]{:S(2)}) copy-start(f32[8,256,512]{2,1,0:T(8,128)} %multiply_reduce_fusion.3) | copy-start | bytes 12582916 | tf_op jit(solution)/shard_map/while
  211.2 8.1 %copy-start = (f32[8,256,512]{2,1,0:T(8,128)S(1)}, f32[8,256,512]{2,1,0:T(8,128)}, u32[]{:S(2)}) copy-start(f32[8,256,512]{2,1,0:T(8,128)} %multiply_reduce_fusion.3) | copy-start | bytes 12582916 | tf_op jit(solution)/shard_map/while
  229.1 8.0 %copy-start = (f32[8,256,512]{2,1,0:T(8,128)S(1)}, f32[8,256,512]{2,1,0:T(8,128)}, u32[]{:S(2)}) copy-start(f32[8,256,512]{2,1,0:T(8,128)} %multiply_reduce_fusion.3) | copy-start | bytes 12582916 | tf_op jit(solution)/shard_map/while
  247.1 8.1 %copy-start = (f32[8,256,512]{2,1,0:T(8,128)S(1)}, f32[8,256,512]{2,1,0:T(8,128)}, u32[]{:S(2)}) copy-start(f32[8,256,512]{2,1,0:T(8,128)} %multiply_reduce_fusion.3) | copy-start | bytes 12582916 | tf_op jit(solution)/shard_map/while
  265.0 8.0 %copy-start = (f32[8,256,512]{2,1,0:T(8,128)S(1)}, f32[8,256,512]{2,1,0:T(8,128)}, u32[]{:S(2)}) copy-start(f32[8,256,512]{2,1,0:T(8,128)} %multiply_reduce_fusion.3) | copy-start | bytes 12582916 | tf_op jit(solution)/shard_map/while
  282.9 8.0 %copy-start = (f32[8,256,512]{2,1,0:T(8,128)S(1)}, f32[8,256,512]{2,1,0:T(8,128)}, u32[]{:S(2)}) copy-start(f32[8,256,512]{2,1,0:T(8,128)} %multiply_reduce_fusion.3) | copy-start | bytes 12582916 | tf_op jit(solution)/shard_map/while
  300.9 8.0 %copy-start = (f32[8,256,512]{2,1,0:T(8,128)S(1)}, f32[8,256,512]{2,1,0:T(8,128)}, u32[]{:S(2)}) copy-start(f32[8,256,512]{2,1,0:T(8,128)} %multiply_reduce_fusion.3) | copy-start | bytes 12582916 | tf_op jit(solution)/shard_map/while
  318.8 8.0 %copy-start = (f32[8,256,512]{2,1,0:T(8,128)S(1)}, f32[8,256,512]{2,1,0:T(8,128)}, u32[]{:S(2)}) copy-start(f32[8,256,512]{2,1,0:T(8,128)} %multiply_reduce_fusion.3) | copy-start | bytes 12582916 | tf_op jit(solution)/shard_map/while
  336.8 8.1 %copy-start = (f32[8,256,512]{2,1,0:T(8,128)S(1)}, f32[8,256,512]{2,1,0:T(8,128)}, u32[]{:S(2)}) copy-start(f32[8,256,512]{2,1,0:T(8,128)} %multiply_reduce_fusion.3) | copy-start | bytes 12582916 | tf_op jit(solution)/shard_map/while
  354.7 8.0 %copy-start = (f32[8,256,512]{2,1,0:T(8,128)S(1)}, f32[8,256,512]{2,1,0:T(8,128)}, u32[]{:S(2)}) copy-start(f32[8,256,512]{2,1,0:T(8,128)} %multiply_reduce_fusion.3) | copy-start | bytes 12582916 | tf_op jit(solution)/shard_map/while
  372.6 8.0 %copy-start = (f32[8,256,512]{2,1,0:T(8,128)S(1)}, f32[8,256,512]{2,1,0:T(8,128)}, u32[]{:S(2)}) copy-start(f32[8,256,512]{2,1,0:T(8,128)} %multiply_reduce_fusion.3) | copy-start | bytes 12582916 | tf_op jit(solution)/shard_map/while
  390.6 8.1 %copy-start = (f32[8,256,512]{2,1,0:T(8,128)S(1)}, f32[8,256,512]{2,1,0:T(8,128)}, u32[]{:S(2)}) copy-start(f32[8,256,512]{2,1,0:T(8,128)} %multiply_reduce_fusion.3) | copy-start | bytes 12582916 | tf_op jit(solution)/shard_map/while
  408.5 8.1 %copy-start = (f32[8,256,512]{2,1,0:T(8,128)S(1)}, f32[8,256,512]{2,1,0:T(8,128)}, u32[]{:S(2)}) copy-start(f32[8,256,512]{2,1,0:T(8,128)} %multiply_reduce_fusion.3) | copy-start | bytes 12582916 | tf_op jit(solution)/shard_map/while
  426.5 8.0 %copy-start = (f32[8,256,512]{2,1,0:T(8,128)S(1)}, f32[8,256,512]{2,1,0:T(8,128)}, u32[]{:S(2)}) copy-start(f32[8,256,512]{2,1,0:T(8,128)} %multiply_reduce_fusion.3) | copy-start | bytes 12582916 | tf_op jit(solution)/shard_map/while
  444.4 8.1 %copy-start = (f32[8,256,512]{2,1,0:T(8,128)S(1)}, f32[8,256,512]{2,1,0:T(8,128)}, u32[]{:S(2)}) copy-start(f32[8,256,512]{2,1,0:T(8,128)} %multiply_reduce_fusion.3) | copy-start | bytes 12582916 | tf_op jit(solution)/shard_map/while
  462.4 8.1 %copy-start = (f32[8,256,512]{2,1,0:T(8,128)S(1)}, f32[8,256,512]{2,1,0:T(8,128)}, u32[]{:S(2)}) copy-start(f32[8,256,512]{2,1,0:T(8,128)} %multiply_reduce_fusion.3) | copy-start | bytes 12582916 | tf_op jit(solution)/shard_map/while
  480.3 8.1 %copy-start = (f32[8,256,512]{2,1,0:T(8,128)S(1)}, f32[8,256,512]{2,1,0:T(8,128)}, u32[]{:S(2)}) copy-start(f32[8,256,512]{2,1,0:T(8,128)} %multiply_reduce_fusion.3) | copy-start | bytes 12582916 | tf_op jit(solution)/shard_map/while
  498.3 8.1 %copy-start = (f32[8,256,512]{2,1,0:T(8,128)S(1)}, f32[8,256,512]{2,1,0:T(8,128)}, u32[]{:S(2)}) copy-start(f32[8,256,512]{2,1,0:T(8,128)} %multiply_reduce_fusion.3) | copy-start | bytes 12582916 | tf_op jit(solution)/shard_map/while
  516.2 8.0 %copy-start = (f32[8,256,512]{2,1,0:T(8,128)S(1)}, f32[8,256,512]{2,1,0:T(8,128)}, u32[]{:S(2)}) copy-start(f32[8,256,512]{2,1,0:T(8,128)} %multiply_reduce_fusion.3) | copy-start | bytes 12582916 | tf_op jit(solution)/shard_map/while
  534.2 8.1 %copy-start = (f32[8,256,512]{2,1,0:T(8,128)S(1)}, f32[8,256,512]{2,1,0:T(8,128)}, u32[]{:S(2)}) copy-start(f32[8,256,512]{2,1,0:T(8,128)} %multiply_reduce_fusion.3) | copy-start | bytes 12582916 | tf_op jit(solution)/shard_map/while
  552.1 8.1 %copy-start = (f32[8,256,512]{2,1,0:T(8,128)S(1)}, f32[8,256,512]{2,1,0:T(8,128)}, u32[]{:S(2)}) copy-start(f32[8,256,512]{2,1,0:T(8,128)} %multiply_reduce_fusion.3) | copy-start | bytes 12582916 | tf_op jit(solution)/shard_map/while
  570.1 8.0 %copy-start = (f32[8,256,512]{2,1,0:T(8,128)S(1)}, f32[8,256,512]{2,1,0:T(8,128)}, u32[]{:S(2)}) copy-start(f32[8,256,512]{2,1,0:T(8,128)} %multiply_reduce_fusion.3) | copy-start | bytes 12582916 | tf_op jit(solution)/shard_map/while
  588.0 8.1 %copy-start = (f32[8,256,512]{2,1,0:T(8,128)S(1)}, f32[8,256,512]{2,1,0:T(8,128)}, u32[]{:S(2)}) copy-start(f32[8,256,512]{2,1,0:T(8,128)} %multiply_reduce_fusion.3) | copy-start | bytes 12582916 | tf_op jit(solution)/shard_map/while
  605.9 8.1 %copy-start = (f32[8,256,512]{2,1,0:T(8,128)S(1)}, f32[8,256,512]{2,1,0:T(8,128)}, u32[]{:S(2)}) copy-start(f32[8,256,512]{2,1,0:T(8,128)} %multiply_reduce_fusion.3) | copy-start | bytes 12582916 | tf_op jit(solution)/shard_map/while
  623.9 8.0 %copy-start = (f32[8,256,512]{2,1,0:T(8,128)S(1)}, f32[8,256,512]{2,1,0:T(8,128)}, u32[]{:S(2)}) copy-start(f32[8,256,512]{2,1,0:T(8,128)} %multiply_reduce_fusion.3) | copy-start | bytes 12582916 | tf_op jit(solution)/shard_map/while
  641.8 8.1 %copy-start = (f32[8,256,512]{2,1,0:T(8,128)S(1)}, f32[8,256,512]{2,1,0:T(8,128)}, u32[]{:S(2)}) copy-start(f32[8,256,512]{2,1,0:T(8,128)} %multiply_reduce_fusion.3) | copy-start | bytes 12582916 | tf_op jit(solution)/shard_map/while
  654.4 24.4 %all-to-all-start.2 = ((f32[32,8,3,256]{3,1,2,0:T(8,128)}), f32[32,8,3,256]{3,1,2,0:T(8,128)S(1)}, u32[]{:S(2)}, u32[]{:S(2)}) async-start(f32[32,8,3,256]{3,1,2,0:T(8,128)} %get-tuple-element.41), calls=%async_computation.2 | async-start | bytes 1572864 | tf_op jit(solution)/shard_map/all_to_all | solution.py:78
where the time goes:
time: 683 us; the launch traced here: 682 us
  matrix products  397 us (58%)
  other arithmetic  136 us (20%)
  local copies, waits for them, and re-layouts  87 us (13%)
  waiting for transfers between devices  41.7 us (6%)
  starting transfers between devices  17.2 us (3%)
    dot_general x32, matrix products, per_group(): jnp.einsum('bpn,bin->bip', kernel_vals, jnp.take(coeffs, slot_ids, axis=0...  237 us
    dot_general x32, matrix products, per_group(): jnp.einsum('bpn,bip->bin', kernel_vals, slot_rows[:, 3:], precision=highest)  145 us
    reduce_sum x32, other arithmetic, kernel(): scaled = jnp.sqrt(jnp.sum(offset * offset, axis=-3))  128 us
    all_to_all x1, waiting for transfers between devices, on_device(): lax.all_to_all(outgoing.reshape(devices, CAP, 6, tile_width), ('row', 'co...  24.8 us
    dynamic_update_slice x32, local copies, waits for them, and re-layouts, on_device(): lax.map(per_group, (slot_ids, arrived.reshape(-1, group_size, 6, tile_wid...  20.1 us
    gather x32, local copies, waits for them, and re-layouts, per_group(): jnp.take(node_coords, slot_ids, axis=0)  18.8 us
    gather x32, local copies, waits for them, and re-layouts, per_group(): jnp.take(coeffs, slot_ids, axis=0)  18.8 us
    scatter x1, local copies, waits for them, and re-layouts, on_device(): jnp.zeros((slot_total, 6, tile_width), jnp.float32).at[slot_of].set(packed)  18.6 us
  transfers between devices with their start and end apart: 3, of which 2 were waited for; matrix products, arithmetic and copies ran while one was open for 6% of the time, Pallas kernels for 0%

commit v1 on v0

v1 whole, which is shorter than its diff:
```python
import functools

import jax
import jax.numpy as jnp
from jax import lax
from jax.experimental import pallas as pl
from jax.experimental.pallas import tpu as pltpu
from jax.sharding import PartitionSpec as P

CAP = 8
BATCH = 128
CHUNK = 256
WINDOW = 64
AXES = ("row", "col")
FAR = 1e9
NT = (((1,), (1,)), ((), ()))
F32 = jnp.float32
BF16 = jnp.bfloat16


def rounded(x):
    return x.astype(BF16).astype(F32)


def split2(x):
    high = rounded(x)
    return high, rounded(x - high)


def split3(x):
    high = rounded(x)
    rest = x - high
    middle = rounded(rest)
    return high, middle, rounded(rest - middle)


def outer_split(x, parts):
    pieces = []
    for _ in range(parts):
        piece = lax.reduce_precision(x, 8, 7)
        pieces.append(piece)
        x = x - piece
    return pieces


def tile_weights(levels):
    levels = levels.astype(F32) + 1.0
    return levels / jnp.sum(levels, axis=0, keepdims=True)


def pack_kernel(local_count, full, ids, points, force, level, out, wanted, slot_of, count):
    devices = out.shape[0]
    tiles, kslots = level.shape[0], level.shape[1]

    @pl.loop(0, devices)
    def _(d):
        count[d] = 0

    if not full:

        @pl.loop(0, devices)
        def _(d):
            out[d] = jnp.zeros(out.shape[1:], F32)
            for j in range(CAP):
                wanted[d * CAP + j] = -1

    @pl.loop(0, tiles)
    def _(t):
        weights = tile_weights(level[t])
        coords = [points[c, pl.ds(t, 1), :] for c in range(3)]
        loads = [weights * (force[c, pl.ds(t, 1), :] * (1.0 / 256.0)) for c in range(3)]
        for k in range(kslots):
            pair = t * kslots + k
            cluster = ids[pair]
            d = cluster // local_count
            j = count[d]
            count[d] = j + 1
            wanted[d * CAP + j] = cluster - d * local_count
            slot_of[pair] = d * CAP + j
            for c in range(3):
                out[d, pl.ds(c * CAP + j, 1), :] = coords[c]
                out[d, pl.ds((3 + c) * CAP + j, 1), :] = loads[c][k : k + 1]


def unpack_kernel(slot_of, back, level, out):
    tiles, kslots = level.shape[0], level.shape[1]

    @pl.loop(0, tiles)
    def _(t):
        weights = tile_weights(level[t])
        sums = [None] * 3
        for k in range(kslots):
            slot = slot_of[t * kslots + k]
            d = slot // CAP
            j = slot - d * CAP
            for c in range(3):
                term = weights[k : k + 1] * back[d, pl.ds(c * CAP + j, 1), :]
                sums[c] = term if k == 0 else sums[c] + term
        for c in range(3):
            out[c, pl.ds(t, 1), :] = sums[c]


def couple_kernel(
    ids,
    boxes,
    arrived,
    node_rows,
    coeff_rows,
    values,
    node_force,
    rank,
    rows,
    packed,
    slot_plan_v,
    cluster_plan_v,
    slot_plan,
    cluster_plan,
    force_sum,
    sems,
):
    groups = arrived.shape[0]
    width = arrived.shape[2]
    batch = groups * CAP
    clusters = node_rows.shape[0]
    step = pl.program_id(0)

    @pl.when(step == 0)
    def _():
        force_sum[...] = jnp.zeros_like(force_sum)

    @pl.loop(0, groups)
    def _(g):
        box = boxes[pl.ds(pl.multiple_of(g * CAP, CAP), CAP), :]
        gap = None
        for c in range(3):
            x = arrived[g, c * CAP : (c + 1) * CAP, :]
            side = jnp.maximum(jnp.maximum(box[:, c : c + 1] - x, x - box[:, 3 + c : 4 + c]), 0.0)
            gap = side * side if c == 0 else gap + side * side
        rank[pl.ds(pl.multiple_of(g * CAP, CAP), CAP), :] = jnp.where(gap < 1.0002, 1.0, 0.0)

    near = rank[...].astype(BF16)
    before = (
        lax.broadcasted_iota(jnp.int32, (width, width), 0)
        < lax.broadcasted_iota(jnp.int32, (width, width), 1)
    ).astype(F32).astype(BF16)
    earlier = jnp.dot(near, before, preferred_element_type=F32)
    rank[...] = jnp.where(near.astype(F32) > 0.5, earlier, -1e6)
    counts = lax.dot_general(jnp.ones((CAP, width), BF16), near, NT, preferred_element_type=F32)
    hits = (lax.broadcasted_iota(jnp.int32, (clusters, batch), 0) == ids[0]).astype(F32)
    hit_counts = hits * counts[0:1]
    before_slot = (
        lax.broadcasted_iota(jnp.int32, (batch, batch), 0)
        < lax.broadcasted_iota(jnp.int32, (batch, batch), 1)
    ).astype(F32).astype(BF16)
    slot_start = jnp.dot(hit_counts.astype(BF16), before_slot, preferred_element_type=F32)
    totals = jnp.sum(hit_counts, axis=1, keepdims=True)
    chunks = jnp.floor((totals + (CHUNK - 1)) * (1.0 / CHUNK))
    chunks = jnp.broadcast_to(chunks, (clusters, 128))
    before_cluster = (
        lax.broadcasted_iota(jnp.int32, (clusters, clusters), 1)
        < lax.broadcasted_iota(jnp.int32, (clusters, clusters), 0)
    ).astype(F32).astype(BF16)
    first_chunk = jnp.dot(before_cluster, chunks.astype(BF16), preferred_element_type=F32)
    offset = jnp.sum(hits * (slot_start + first_chunk[:, 0:1] * CHUNK), axis=0, keepdims=True)
    slot_plan_v[0:1, :] = offset.astype(jnp.int32)
    slot_plan_v[1:2, :] = counts[0:1].astype(jnp.int32)
    lane = lax.broadcasted_iota(jnp.int32, (clusters, 128), 1)
    cluster_plan_v[...] = jnp.where(lane == 0, first_chunk, chunks).astype(jnp.int32)
    copies = [
        pltpu.make_async_copy(slot_plan_v, slot_plan, sems.at[0]),
        pltpu.make_async_copy(cluster_plan_v, cluster_plan, sems.at[1]),
    ]
    for copy in copies:
        copy.start()
    for copy in copies:
        copy.wait()
    total_chunks = cluster_plan[clusters - 1, 0] + cluster_plan[clusters - 1, 1]

    @pl.loop(0, total_chunks + 1)
    def _(j):
        packed[pl.ds(pl.multiple_of(j * CHUNK, CHUNK), CHUNK), :] = jnp.zeros((CHUNK, 128), F32)

    target = lax.broadcasted_iota(jnp.int32, (WINDOW, 1), 0).astype(F32)

    def place_of(g, i):
        slot = g * CAP + i
        start = slot_plan[0, slot]
        base = (start // 8) * 8
        lead = start - base
        blocks = (lead + slot_plan[1, slot] + (WINDOW - 1)) // WINDOW
        return rank[pl.ds(slot, 1), :], base, lead, blocks

    def selection(ranks, lead, block):
        shift = (lead - block * WINDOW).astype(F32)
        return jnp.where(ranks + shift == target, 1.0, 0.0).astype(BF16)

    def window_of(base, block):
        return pl.ds(pl.multiple_of(base + block * WINDOW, 8), WINDOW)

    @pl.loop(0, groups)
    def _(g):
        box = boxes[pl.ds(pl.multiple_of(g * CAP, CAP), CAP), :]
        x = [arrived[g, c * CAP : (c + 1) * CAP, :] - box[:, 6 + c : 7 + c] for c in range(3)]
        parts = [split3(v) for v in x]
        square = split3(x[0] * x[0] + x[1] * x[1] + x[2] * x[2])
        loads = [split2(arrived[g, (3 + c) * CAP : (4 + c) * CAP, :]) for c in range(3)]
        column = [parts[c][p] for p in (0, 1, 2, 0, 1, 0) for c in range(3)]
        column += list(square) + [jnp.ones_like(x[0])] * 3
        column += [loads[c][p] for p in range(2) for c in range(3)]
        column += [jnp.zeros_like(x[0])] * 2
        for i, tile in enumerate(column):
            rows[:, i * CAP : (i + 1) * CAP, :] = jnp.stack(
                [tile[:, h * 128 : (h + 1) * 128] for h in range(width // 128)]
            )
        places = [place_of(g, i) for i in range(CAP)]

        def slot_rows(i):
            return jnp.concatenate(
                [rows[h, pl.ds(i, 32, stride=CAP), :] for h in range(width // 128)], axis=1
            ).astype(BF16)

        moved = [
            lax.dot_general(
                selection(places[i][0], places[i][2], 0), slot_rows(i), NT, preferred_element_type=F32
            )
            for i in range(CAP)
        ]
        for i in range(CAP):
            packed[window_of(places[i][1], 0), 0:32] += moved[i]
        for i in range(CAP):
            ranks, base, lead, blocks = places[i]

            @pl.loop(1, blocks)
            def _(block):
                packed[window_of(base, block), 0:32] += lax.dot_general(
                    selection(ranks, lead, block), slot_rows(i), NT, preferred_element_type=F32
                )

    @pl.loop(0, clusters)
    def _(c):
        first = cluster_plan[c, 0]

        @pl.loop(0, cluster_plan[c, 1])
        def _(j):
            where = pl.ds(pl.multiple_of((first + j) * CHUNK, CHUNK), CHUNK)
            points = packed[where, :]
            square = jnp.dot(points[:, 0:32].astype(BF16), node_rows[c], preferred_element_type=F32)
            square = jnp.maximum(square, 1e-30)
            rest = jnp.maximum(4.0 - square * lax.rsqrt(square), 0.0)
            rest2 = rest * rest
            kernel = (rest2 * rest2) * (5.0 - rest)
            high = kernel.astype(BF16)
            low = (kernel - high.astype(F32)).astype(BF16)
            loads = jnp.transpose(points)[24:32].astype(BF16)
            packed[where, 0:16] = lax.dot_general(
                high, coeff_rows[c], NT, preferred_element_type=F32
            ) + lax.dot_general(low, coeff_rows[c], NT, preferred_element_type=F32)
            force_sum[c] += jnp.dot(loads, high, preferred_element_type=F32) + jnp.dot(
                loads, low, preferred_element_type=F32
            )

    @pl.loop(0, groups)
    def _(g):
        places = [place_of(g, i) for i in range(CAP)]

        def spread(place, block):
            ranks, base, lead, _ = place
            rows_t = jnp.transpose(packed[window_of(base, block), :])
            high, middle, low = split3(rows_t[0:8] + rows_t[8:16])
            stacked = jnp.concatenate([high, middle, low], axis=0).astype(BF16)
            moved = jnp.dot(stacked, selection(ranks, lead, block), preferred_element_type=F32)
            return moved[0:8] + moved[8:16] + moved[16:24]

        found = [spread(places[i], 0) for i in range(CAP)]
        for i in range(CAP):
            for c in range(3):
                values[g, c * CAP + i : c * CAP + i + 1, :] = found[i][c : c + 1]
        for i in range(CAP):

            @pl.loop(1, places[i][3])
            def _(block):
                more = spread(places[i], block)
                for c in range(3):
                    values[g, c * CAP + i : c * CAP + i + 1, :] += more[c : c + 1]

    @pl.when(step == pl.num_programs(0) - 1)
    def _():
        for c in range(clusters):
            both = force_sum[c]
            for i in range(3):
                node_force[i, c : c + 1, :] = both[i : i + 1] + both[3 + i : 4 + i]


def vmem():
    return pl.BlockSpec(memory_space=pltpu.VMEM)


def smem():
    return pl.BlockSpec(memory_space=pltpu.SMEM)


def on_device(point_coords, fluid_force, tile_clusters, pu_level, node_coords, node_disp, inverse):
    highest = lax.Precision.HIGHEST
    devices = lax.axis_size(AXES)
    slot_total = devices * CAP
    tile_total, kslots = tile_clusters.shape
    pair_total = tile_total * kslots
    local_count, _, node_count = node_coords.shape
    width = point_coords.shape[2]
    batch = min(BATCH, slot_total)
    groups = batch // CAP

    outgoing, wanted, slot_of = pl.pallas_call(
        functools.partial(pack_kernel, local_count, pair_total == slot_total),
        out_shape=(
            jax.ShapeDtypeStruct((devices, 6 * CAP, width), F32),
            jax.ShapeDtypeStruct((slot_total,), jnp.int32),
            jax.ShapeDtypeStruct((pair_total,), jnp.int32),
        ),
        in_specs=[smem(), vmem(), vmem(), vmem()],
        out_specs=(vmem(), smem(), smem()),
        scratch_shapes=[pltpu.SMEM((devices,), jnp.int32)],
        name="pack",
    )(
        tile_clusters.reshape(-1),
        jnp.transpose(point_coords, (1, 0, 2)),
        jnp.transpose(fluid_force, (1, 0, 2)),
        pu_level,
    )
    asked = lax.all_to_all(
        wanted.reshape(devices, CAP), AXES, split_axis=0, concat_axis=0, tiled=True
    ).reshape(slot_total)
    arrived = lax.all_to_all(outgoing, AXES, split_axis=0, concat_axis=0, tiled=True)

    coeffs = jnp.einsum("cin,cnm->cim", node_disp, inverse, precision=highest) * (1.0 / 256.0)
    high, low = outer_split(coeffs, 2)
    gap5 = jnp.zeros((local_count, 5, node_count), F32)
    coeff_rows = jnp.concatenate((high, gap5, low, gap5), axis=1).astype(BF16)
    least = jnp.min(node_coords, axis=2)
    most = jnp.max(node_coords, axis=2)
    centre = 0.5 * (least + most)
    nodes = node_coords - centre[:, :, None]
    near = [-32.0 * piece for piece in outer_split(nodes, 3)]
    square = [16.0 * p for p in outer_split(jnp.sum(nodes * nodes, axis=1, keepdims=True), 3)]
    sixteen = jnp.full((local_count, 3, node_count), 16.0, F32)
    rows = [near[0]] * 3 + [near[1]] * 2 + [near[2], sixteen] + square
    rows.append(jnp.zeros((local_count, 8, node_count), F32))
    node_rows = jnp.concatenate(rows, axis=1).astype(BF16)

    table = jnp.concatenate((least, most, centre), axis=1)
    chosen = asked[:, None] == jnp.arange(local_count, dtype=jnp.int32)[None, :]
    boxes = jnp.sum(jnp.where(chosen[:, :, None], table[None], 0.0), axis=1)
    nowhere = jnp.array([FAR] * 3 + [-FAR] * 3 + [0.0] * 3, F32)
    boxes = jnp.where(asked[:, None] < 0, nowhere[None], boxes)

    spare = local_count * CHUNK + CHUNK + 2 * WINDOW
    values, node_force = pl.pallas_call(
        couple_kernel,
        grid=(slot_total // batch,),
        out_shape=(
            jax.ShapeDtypeStruct((devices, 3 * CAP, width), F32),
            jax.ShapeDtypeStruct((3, local_count, node_count), F32),
        ),
        in_specs=[
            pl.BlockSpec((1, 1, batch), lambda i: (i, 0, 0)),
            pl.BlockSpec((batch, 9), lambda i: (i, 0)),
            pl.BlockSpec((groups, 6 * CAP, width), lambda i: (i, 0, 0)),
            vmem(),
            vmem(),
        ],
        out_specs=(
            pl.BlockSpec((groups, 3 * CAP, width), lambda i: (i, 0, 0)),
            pl.BlockSpec((3, local_count, node_count), lambda i: (0, 0, 0)),
        ),
        scratch_shapes=[
            pltpu.VMEM((batch, width), F32),
            pltpu.VMEM((width // 128, 32 * CAP, 128), F32),
            pltpu.VMEM((batch * width + spare, 128), F32),
            pltpu.VMEM((8, batch), jnp.int32),
            pltpu.VMEM((local_count, 128), jnp.int32),
            pltpu.SMEM((8, batch), jnp.int32),
            pltpu.SMEM((local_count, 128), jnp.int32),
            pltpu.VMEM((local_count, 8, node_count), F32),
            pltpu.SemaphoreType.DMA((2,)),
        ],
        compiler_params=pltpu.CompilerParams(vmem_limit_bytes=48 * 1024 * 1024),
        name="couple",
    )(asked.reshape(-1, 1, batch), boxes, arrived, node_rows, coeff_rows)

    back = lax.all_to_all(values, AXES, split_axis=0, concat_axis=0, tiled=True)
    point_disp = pl.pallas_call(
        unpack_kernel,
        out_shape=jax.ShapeDtypeStruct((3, tile_total, width), F32),
        in_specs=[smem(), vmem(), vmem()],
        out_specs=vmem(),
        name="unpack",
    )(slot_of, back, pu_level)
    return jnp.transpose(point_disp, (1, 0, 2)), jnp.transpose(node_force, (1, 0, 2))


def solution(mesh):
    placed = (
        P(AXES, None, None),
        P(AXES, None, None),
        P(AXES, None),
        P(AXES, None, None),
        P(AXES, None, None),
        P(AXES, None, None),
        P(AXES, None, None),
    )
    return jax.shard_map(
        on_device,
        mesh=mesh,
        in_specs=placed,
        out_specs=(P(AXES, None, None), P(AXES, None, None)),
        check_vma=False,
    )
```

time: 683 us -> 162 us (0.24)
  matrix products: 397 us -> 11.7 us
  other arithmetic: 136 us -> 3.27 us
  local copies, waits for them, and re-layouts: 87 us -> 4.13 us
  Pallas kernels: 0 us -> 75 us
  blocking collectives: 0 us -> 43.7 us
  waiting for transfers between devices: 41.7 us -> 20.7 us
  starting transfers between devices: 17.2 us -> 2.69 us
    dot_general x66 -> x1, matrix products: 397 us -> 11.7 us  [on_device(): jnp.einsum('cin,cnm->cim', node_disp, inverse, precision=highest)]
    reduce_sum x35 -> x2, other arithmetic: 129 us -> 1.08 us  [the longest x1 0.98 us: on_device(): jnp.sum(nodes * nodes, axis=1, keepdims=True)]
    pallas_call x0 -> x3, Pallas kernels: none -> 75 us  [the longest x1 61.8 us: on_device(): pl.pallas_call(couple_kernel, grid=(slot_total // batch,), out_shape=(jax...]
    all_to_all x0 -> x2, blocking collectives: none -> 43.7 us  [the longest x1 29.4 us: on_device(): back = lax.all_to_all(values, AXES, split_axis=0, concat_axis=0, tiled=True)]
    gather x65 -> x0, local copies, waits for them, and re-layouts: 38.9 us -> none  [the longest x32 18.8 us: per_group(): jnp.take(node_coords, slot_ids, axis=0)]
    all_to_all x3 -> x1, waiting for transfers between devices: 41.7 us -> 20.7 us  [on_device(): lax.all_to_all(outgoing, AXES, split_axis=0, concat_axis=0, tiled=True)]
    dynamic_update_slice x32 -> x0, local copies, waits for them, and re-layouts: 20.1 us -> none  [on_device(): lax.map(per_group, (slot_ids, arrived.reshape(-1, group_size, 6, tile_wid...]
    scatter x1 -> x0, local copies, waits for them, and re-layouts: 18.6 us -> none  [on_device(): jnp.zeros((slot_total, 6, tile_width), jnp.float32).at[slot_of].set(packed)]
  transfers between devices with their start and end apart: 3 -> 1, of which waited for: 2 -> 1; matrix products, arithmetic and copies ran while one was open for 6% -> 10% of each run, Pallas kernels for 0% -> 0%
where the time goes in v1:
time: 162 us
  Pallas kernels  75 us (46%)
  blocking collectives  43.7 us (27%)
  waiting for transfers between devices  20.7 us (13%)
  matrix products  11.7 us (7%)
  local copies, waits for them, and re-layouts  4.13 us (3%)
  other arithmetic  3.27 us (2%)
  starting transfers between devices  2.69 us (2%)
    pallas_call x1, Pallas kernels, on_device(): pl.pallas_call(couple_kernel, grid=(slot_total // batch,), out_shape=(jax...  61.8 us
    all_to_all x1, blocking collectives, on_device(): back = lax.all_to_all(values, AXES, split_axis=0, concat_axis=0, tiled=True)  29.4 us
    all_to_all x1, waiting for transfers between devices, on_device(): lax.all_to_all(outgoing, AXES, split_axis=0, concat_axis=0, tiled=True)  20.7 us
    all_to_all x1, blocking collectives, on_device(): lax.all_to_all(wanted.reshape(devices, CAP), AXES, split_axis=0, concat_a...  14.3 us
    dot_general x1, matrix products, on_device(): jnp.einsum('cin,cnm->cim', node_disp, inverse, precision=highest)  11.7 us
    pallas_call x1, Pallas kernels, on_device(): pl.pallas_call(functools.partial(pack_kernel, local_count, pair_total ==...  8.18 us
    pallas_call x1, Pallas kernels, on_device(): pl.pallas_call(unpack_kernel, out_shape=jax.ShapeDtypeStruct((3, tile_tot...  4.99 us
  transfers between devices with their start and end apart: 1, of which 1 were waited for; matrix products, arithmetic and copies ran while one was open for 10% of the time, Pallas kernels for 0%

profile of v1, /device:TPU:0, one launch (start us, length us, event | category | flops | bytes accessed | tf_op | source)
XLA Modules:
  0.0 162.0 jit_solution(1083467727097464398)
XLA Ops:
  0.6 0.0 copy-start
  0.6 0.8 copy.30
  1.4 0.7 reshape.97.ids
  2.1 8.2 %pack.1 = (f32[32,48,256]{2,1,0:T(8,128)}, s32[256]{0:T(256)}, s32[256]{0:T(256)}) custom-call(s32[256]{0:T(256)} %reshape.97.ids, f32[3,32,256]{2,1,0:T(8,128)} %bitcast.10, f32[3,32,256]{2,1,0:T(8,128)} %bitcast.11, s32[32,8,256]{2,1,0:T(8,128)} %level.3), custom_call_target="tpu_custom_call" | custom-call | tf_op jit(solution)/shard_map/pack/pallas_call | solution.py:313
  10.3 0.8 all_to_all.12
  11.0 14.3 %all_to_all.19 = s32[32,1,8]{2,1,0:T(1,128)S(1)} all-to-all(s32[32,1,8]{2,1,0:T(1,128)S(1)} %bitcast.13), channel_id=1, replica_groups=mesh['row'=4,'col'=8] {'row','col'}, dimensions={0} | all-to-all | bytes 2048 | tf_op jit(solution)/shard_map/all_to_all | solution.py:330
  25.3 2.7 %all-to-all-start.1 = ((f32[32,48,256]{2,1,0:T(8,128)}), f32[32,48,256]{2,1,0:T(8,128)S(1)}, u32[]{:S(2)}, u32[]{:S(2)}) async-start(f32[32,48,256]{2,1,0:T(8,128)} %get-tuple-element.9), calls=%async_computation.1 | async-start | bytes 3145728 | tf_op jit(solution)/shard_map/all_to_all | solution.py:333
  28.0 1.0 fusion.13
  29.0 1.0 multiply_reduce_fusion
  30.0 0.1 fusion.12
  30.1 0.1 fusion.4
  30.3 1.1 concatenate.12.node_rows
  31.4 11.7 %reduce-precision_convert_fusion = (bf16[16,3,512]{2,1,0:T(4,128)(2,1)S(1)}, bf16[16,3,512]{2,1,0:T(4,128)(2,1)S(1)}) fusion(f32[16,512,512]{2,1,0:T(8,128)} %param.14, f32[16,3,512]{2,0,1:T(8,128)} %param.13), kind=kOutput, calls=%fused_computation.3 | convolution fusion | flops 151142400 | bytes 16973824 | tf_op jit(solution)/shard_map/cin,cnm->cim/dot_general | solution.py:335
  43.1 0.2 pad_maximum_fusion.coeff_rows
  43.3 0.5 broadcast.75
  43.8 0.7 reduce.5
  44.5 0.1 reshape_reshape.3
  44.6 0.1 broadcast_in_dim_reshape.4
  44.7 0.1 select_reduce_fusion
  44.8 0.1 copy.32
  45.0 0.0 copy-done
  45.0 0.1 broadcast_select_fusion.boxes
  45.1 20.7 %all-to-all-done.1.arrived = f32[32,48,256]{2,1,0:T(8,128)S(1)} async-done(((f32[32,48,256]{2,1,0:T(8,128)}), f32[32,48,256]{2,1,0:T(8,128)S(1)}, u32[]{:S(2)}, u32[]{:S(2)}) %all-to-all-start.1) | async-done | bytes 1572896 | tf_op jit(solution)/shard_map/all_to_all | solution.py:333
  65.8 61.8 %couple.1 = (f32[32,24,256]{2,1,0:T(8,128)S(1)}, f32[3,16,512]{2,1,0:T(8,128)}) custom-call(s32[2,1,128]{2,1,0:T(1,128)S(1)} %bitcast.8, f32[256,9]{1,0:T(8,128)S(1)} %broadcast_select_fusion.boxes, f32[32,48,256]{2,1,0:T(8,128)S(1)} %all-to-all-done.1.arrived, bf16[16,32,512]{2,1,0:T(8,128)(2,1)S(1)} %concatenate.12.node_rows, ...), custom_call_target="tpu_custom_call" | custom-call | tf_op jit(solution)/shard_map/couple/pallas_call | solution.py:357
  127.6 29.4 %all_to_all.20.back = f32[32,24,256]{2,1,0:T(8,128)} all-to-all(f32[32,24,256]{2,1,0:T(8,128)S(1)} %get-tuple-element.10), channel_id=1, replica_groups=mesh['row'=4,'col'=8] {'row','col'}, dimensions={0} | all-to-all | bytes 1572864 | tf_op jit(solution)/shard_map/all_to_all | solution.py:390
  157.0 5.0 %unpack.1 = f32[3,32,256]{2,1,0:T(8,128)} custom-call(s32[256]{0:T(256)} %get-tuple-element.7.slot_of, f32[32,24,256]{2,1,0:T(8,128)} %all_to_all.20.back, s32[32,8,256]{2,1,0:T(8,128)} %level.3), custom_call_target="tpu_custom_call" | custom-call | tf_op jit(solution)/shard_map/unpack/pallas_call | solution.py:391
  (7 shorter events, 0.1 us)
Async XLA Ops:
  0.6 44.3 %copy-start = (f32[9]{0:T(128)S(1)}, f32[9]{0:T(128)}, u32[]{:S(2)}) copy-start(f32[9]{0:T(128)} %constant.25.clone) | copy-start | bytes 112
  25.3 40.5 %all-to-all-start.1 = ((f32[32,48,256]{2,1,0:T(8,128)}), f32[32,48,256]{2,1,0:T(8,128)S(1)}, u32[]{:S(2)}, u32[]{:S(2)}) async-start(f32[32,48,256]{2,1,0:T(8,128)} %get-tuple-element.9), calls=%async_computation.1 | async-start | bytes 3145728 | tf_op jit(solution)/shard_map/all_to_all | solution.py:333

commit v2 on v0

v2 whole, which is shorter than its diff:
```python
import functools

import jax
import jax.numpy as jnp
from jax import lax
from jax.experimental import pallas as pl
from jax.experimental.pallas import tpu as pltpu
from jax.sharding import PartitionSpec as P

CAP = 8
PARTS = 2
SHARE = CAP // PARTS
GROUP = 8
BATCH = 128
CHUNK = 256
WINDOW = 96
LANES = 128
AXES = ("row", "col")
NT = (((1,), (1,)), ((), ()))
F32 = jnp.float32
BF16 = jnp.bfloat16


def rounded(x):
    return x.astype(BF16).astype(F32)


def split2(x):
    high = rounded(x)
    return high, rounded(x - high)


def split3(x):
    high = rounded(x)
    rest = x - high
    middle = rounded(rest)
    return high, middle, rounded(rest - middle)


def outer_split(x, parts):
    pieces = []
    for _ in range(parts):
        piece = lax.reduce_precision(x, 8, 7)
        pieces.append(piece)
        x = x - piece
    return pieces


def tile_weights(levels):
    levels = levels.astype(F32) + 1.0
    return levels / jnp.sum(levels, axis=0, keepdims=True)


def iota(shape, axis):
    return lax.broadcasted_iota(jnp.int32, shape, axis)


def as_bf16(mask):
    return mask.astype(F32).astype(BF16)


def copy_slots(part, pair_of, points, loads, out):
    devices = out.shape[0]
    halves = points.shape[2] // LANES
    kslots = loads.shape[1] // points.shape[1]

    @pl.loop(0, devices)
    def _(d):
        for j in range(SHARE):
            pair = jnp.maximum(pair_of[d * CAP + part * SHARE + j], 0)
            tile = pair // kslots
            for c in range(6):
                whole = points[c, pl.ds(tile, 1), :] if c < 3 else loads[c - 3, pl.ds(pair, 1), :]
                for h in range(halves):
                    row = c * GROUP + h * SHARE + j
                    out[d, row : row + 1, :] = whole[:, h * LANES : (h + 1) * LANES]


def first_pack_kernel(local_count, full, ids, points, force, level, out, loads, pair_of, count):
    devices = out.shape[0]
    tiles, kslots = level.shape[0], level.shape[1]

    @pl.loop(0, devices)
    def _(d):
        count[d] = 0
        if not full:
            out[d, 6 * GROUP : 7 * GROUP, :] = jnp.full((CAP, LANES), -1.0, F32)
            for j in range(CAP):
                pair_of[d * CAP + j] = -1

    @pl.loop(0, tiles)
    def _(t):
        weights = tile_weights(level[t])
        for c in range(3):
            where = pl.ds(pl.multiple_of(t * kslots, kslots), kslots)
            loads[c, where, :] = weights * (force[c, pl.ds(t, 1), :] * (1.0 / 256.0))
        for k in range(kslots):
            pair = t * kslots + k
            cluster = ids[pair]
            d = cluster // local_count
            j = count[d]
            count[d] = j + 1
            pair_of[d * CAP + j] = pair
            own = (cluster - d * local_count).astype(F32)
            out[d, pl.ds(6 * GROUP + j, 1), :] = jnp.full((1, LANES), own)

    copy_slots(0, pair_of, points, loads, out)


def next_pack_kernel(part, pair_of, points, loads, out):
    copy_slots(part, pair_of, points, loads, out)


def unpack_kernel(pair_of, *refs):
    backs, level, out, rows = refs[:PARTS], refs[PARTS], refs[PARTS + 1], refs[PARTS + 2]
    tiles, kslots = level.shape[0], level.shape[1]
    halves = out.shape[2] // LANES
    devices = backs[0].shape[0]

    @pl.loop(0, devices)
    def _(d):
        for slot in range(CAP):
            pair = pair_of[d * CAP + slot]
            pair = jnp.where(pair < 0, tiles * kslots, pair)
            back, j = backs[slot // SHARE], slot % SHARE
            for c in range(3):
                pieces = [
                    back[d, c * GROUP + h * SHARE + j : c * GROUP + h * SHARE + j + 1, :]
                    for h in range(halves)
                ]
                rows[c, pl.ds(pair, 1), :] = jnp.concatenate(pieces, axis=1)

    @pl.loop(0, tiles)
    def _(t):
        weights = tile_weights(level[t])
        where = pl.ds(pl.multiple_of(t * kslots, kslots), kslots)
        for c in range(3):
            out[c, pl.ds(t, 1), :] = jnp.sum(weights * rows[c, where, :], axis=0, keepdims=True)


def couple_kernel(part, *refs):
    refs = list(refs)
    first, last = part == 0, part == PARTS - 1
    id_tiles, arrived, table, node_rows, coeff_rows = refs[:5]
    del refs[:5]
    earlier_force = None if first else refs.pop(0)
    values, node_force = refs[:2]
    (
        rank,
        id_rows,
        boxes,
        rows,
        packed,
        even,
        odd,
        slot_plan_v,
        cluster_plan_v,
        slot_plan,
        cluster_plan,
        cluster_of,
        force_sum,
        sems,
    ) = refs[2:]
    sources = arrived.shape[0]
    batch = sources * SHARE
    groups = batch // GROUP
    per_group = GROUP // SHARE
    halves = GROUP // SHARE
    width = halves * LANES
    clusters = node_rows.shape[0]
    step = pl.program_id(0)

    @pl.when(step == 0)
    def _():
        if first:
            force_sum[...] = jnp.zeros_like(force_sum)
        else:
            force_sum[...] = earlier_force[...]

    def group_rows(g):
        return pl.ds(pl.multiple_of(g * GROUP, GROUP), GROUP)

    @pl.loop(0, groups)
    def _(g):
        id_rows[group_rows(g), :] = jnp.concatenate(
            [
                id_tiles[g * per_group + i, part * SHARE : (part + 1) * SHARE, :]
                for i in range(per_group)
            ],
            axis=0,
        )

    lane = iota((1, LANES), 1)
    own = id_rows[...]
    thrice = (own == (lane % clusters).astype(F32)) & (lane < 3 * clusters)
    boxes[...] = jnp.dot(as_bf16(thrice), table[...], preferred_element_type=F32)

    def slot_tiles(box, i):
        return jnp.concatenate([box[i * SHARE : (i + 1) * SHARE]] * halves, axis=0)

    @pl.loop(0, groups)
    def _(g):
        found = []
        for i in range(per_group):
            d = g * per_group + i
            box = slot_tiles(boxes[group_rows(g), :], i)
            gap = jnp.where(slot_tiles(id_rows[group_rows(g), :], i) < 0.0, 4.0, 0.0)
            for c in range(3):
                x = arrived[d, c * GROUP : (c + 1) * GROUP, :]
                side = jnp.maximum(box[:, c : c + 1] - x, x - box[:, 3 + c : 4 + c])
                side = jnp.maximum(side, 0.0)
                gap = gap + side * side
            found.append(jnp.where(gap < 1.0002, 1.0, 0.0))
        for h in range(halves):
            rank[group_rows(g), h * LANES : (h + 1) * LANES] = jnp.concatenate(
                [tile[h * SHARE : (h + 1) * SHARE] for tile in found], axis=0
            )

    near = rank[...].astype(BF16)
    before = as_bf16(iota((width, width), 0) < iota((width, width), 1))
    earlier = jnp.dot(near, before, preferred_element_type=F32)
    rank[...] = jnp.where(near.astype(F32) > 0.5, earlier, -1e6)
    counts = lax.dot_general(jnp.ones((8, width), BF16), near, NT, preferred_element_type=F32)
    pick = as_bf16(iota((clusters, LANES), 0) == iota((clusters, LANES), 1))
    hits = lax.dot_general(
        pick, as_bf16(own == lane.astype(F32)), NT, preferred_element_type=F32
    )
    hit_counts = hits * counts[0:1]
    before_slot = as_bf16(iota((batch, batch), 0) < iota((batch, batch), 1))
    slot_start = jnp.dot(hit_counts.astype(BF16), before_slot, preferred_element_type=F32)
    totals = jnp.sum(hit_counts, axis=1, keepdims=True)
    chunks = jnp.floor((totals + (CHUNK - 1)) * (1.0 / CHUNK))
    chunks = jnp.broadcast_to(chunks, (clusters, LANES))
    before_cluster = as_bf16(iota((clusters, clusters), 1) < iota((clusters, clusters), 0))
    first_chunk = jnp.dot(before_cluster, chunks.astype(BF16), preferred_element_type=F32)
    offset = jnp.sum(hits * (slot_start + first_chunk[:, 0:1] * CHUNK), axis=0, keepdims=True)
    slot_plan_v[0:1, :] = offset.astype(jnp.int32)
    slot_plan_v[1:2, :] = counts[0:1].astype(jnp.int32)
    cluster_plan_v[...] = jnp.where(lane == 0, first_chunk, chunks).astype(jnp.int32)
    copies = [
        pltpu.make_async_copy(slot_plan_v, slot_plan, sems.at[0]),
        pltpu.make_async_copy(cluster_plan_v, cluster_plan, sems.at[1]),
    ]
    for copy in copies:
        copy.start()
    for copy in copies:
        copy.wait()
    total_chunks = cluster_plan[clusters - 1, 0] + cluster_plan[clusters - 1, 1]

    @pl.loop(0, clusters)
    def _(c):
        @pl.loop(0, cluster_plan[c, 1])
        def _(j):
            cluster_of[cluster_plan[c, 0] + j] = c

    def chunk_rows(j):
        return pl.ds(pl.multiple_of(j * CHUNK, CHUNK), CHUNK)

    @pl.loop(0, total_chunks + 3)
    def _(j):
        packed[chunk_rows(j), :] = jnp.zeros((CHUNK, LANES), F32)

    for extra in range(3):
        cluster_of[total_chunks + extra] = 0

    target = iota((WINDOW, 1), 0).astype(F32)

    def places_of(g):
        places = []
        for i in range(GROUP):
            slot = g * GROUP + i
            start = slot_plan[0, slot]
            base = (start // 8) * 8
            lead = start - base
            blocks = (lead + slot_plan[1, slot] + (WINDOW - 1)) // WINDOW
            places.append((rank[pl.ds(slot, 1), :], base, lead, blocks))
        most = places[0][3]
        for place in places[1:]:
            most = jnp.maximum(most, place[3])
        return places, most

    def selection(place, block):
        shift = (place[2] - block * WINDOW).astype(F32)
        return jnp.where(place[0] + shift == target, 1.0, 0.0).astype(BF16)

    def window_of(place, block):
        return pl.ds(pl.multiple_of(place[1] + block * WINDOW, 8), WINDOW)

    @pl.loop(0, groups)
    def _(g):
        for i in range(per_group):
            d = g * per_group + i
            box = slot_tiles(boxes[group_rows(g), :], i)
            x = [
                arrived[d, c * GROUP : (c + 1) * GROUP, :] - box[:, 6 + c : 7 + c] for c in range(3)
            ]
            parts = [split3(v) for v in x]
            square = split3(x[0] * x[0] + x[1] * x[1] + x[2] * x[2])
            loads = [split2(arrived[d, (3 + c) * GROUP : (4 + c) * GROUP, :]) for c in range(3)]
            column = [parts[c][p] for p in (0, 1, 2, 0, 1, 0) for c in range(3)]
            column += list(square) + [jnp.ones_like(x[0])] * 3
            column += [loads[c][p] for p in range(2) for c in range(3)]
            column += [jnp.zeros_like(x[0])] * 2
            for n, tile in enumerate(column):
                rows[i, n * GROUP : (n + 1) * GROUP, :] = tile
        places, most = places_of(g)

        def gathered(i, block):
            source = rows.at[i // SHARE]
            pieces = [
                source[pl.ds(h * SHARE + i % SHARE, 32, stride=GROUP), :] for h in range(halves)
            ]
            return lax.dot_general(
                selection(places[i], block),
                jnp.concatenate(pieces, axis=1).astype(BF16),
                NT,
                preferred_element_type=F32,
            )

        moved = [gathered(i, 0) for i in range(GROUP)]
        for i in range(GROUP):
            packed[window_of(places[i], 0), 0:32] += moved[i]

        @pl.when(most > 1)
        def _():
            for i in range(GROUP):

                @pl.loop(1, places[i][3])
                def _(block):
                    packed[window_of(places[i], block), 0:32] += gathered(i, block)

    def distances(j, squares):
        squares[...] = jnp.dot(
            packed[chunk_rows(j), 0:32].astype(BF16),
            node_rows[cluster_of[j]],
            preferred_element_type=F32,
        )

    def contract(j, squares):
        c = cluster_of[j]
        square = jnp.maximum(squares[...], 1e-30)
        rest = jnp.maximum(4.0 - square * lax.rsqrt(square), 0.0)
        rest2 = rest * rest
        kernel = (rest2 * rest2) * (5.0 - rest)
        high = kernel.astype(BF16)
        low = (kernel - high.astype(F32)).astype(BF16)
        loads = jnp.transpose(packed[chunk_rows(j), :])[24:32].astype(BF16)
        packed[chunk_rows(j), 0:16] = lax.dot_general(
            high, coeff_rows[c], NT, preferred_element_type=F32
        ) + lax.dot_general(low, coeff_rows[c], NT, preferred_element_type=F32)
        force_sum[c] += jnp.dot(loads, high, preferred_element_type=F32) + jnp.dot(
            loads, low, preferred_element_type=F32
        )

    distances(0, even)

    @pl.loop(0, (total_chunks + 1) // 2)
    def _(j):
        distances(2 * j + 1, odd)
        contract(2 * j, even)
        distances(2 * j + 2, even)
        contract(2 * j + 1, odd)

    @pl.loop(0, groups)
    def _(g):
        places, most = places_of(g)

        def spread(i, block):
            rows_t = jnp.transpose(packed[window_of(places[i], block), :])
            high, middle, low = split3(rows_t[0:8] + rows_t[8:16])
            stacked = jnp.concatenate([high, middle, low], axis=0).astype(BF16)
            moved = jnp.dot(stacked, selection(places[i], block), preferred_element_type=F32)
            return moved[0:8] + moved[8:16] + moved[16:24]

        def pieces_of(i, found):
            d = g * per_group + i // SHARE
            for c in range(3):
                for h in range(halves):
                    row = c * GROUP + h * SHARE + i % SHARE
                    yield d, row, found[c : c + 1, h * LANES : (h + 1) * LANES]

        spreads = [spread(i, 0) for i in range(GROUP)]
        for i in range(GROUP):
            for d, row, piece in pieces_of(i, spreads[i]):
                values[d, row : row + 1, :] = piece

        @pl.when(most > 1)
        def _():
            for i in range(GROUP):

                @pl.loop(1, places[i][3])
                def _(block):
                    for d, row, piece in pieces_of(i, spread(i, block)):
                        values[d, row : row + 1, :] += piece

    @pl.when(step == pl.num_programs(0) - 1)
    def _():
        if last:
            for c in range(clusters):
                both = force_sum[c]
                for i in range(3):
                    node_force[i, c : c + 1, :] = both[i : i + 1] + both[3 + i : 4 + i]
        else:
            node_force[...] = force_sum[...]


def vmem():
    return pl.BlockSpec(memory_space=pltpu.VMEM)


def smem():
    return pl.BlockSpec(memory_space=pltpu.SMEM)


def couple(part, id_source, arrived, table, node_rows, coeff_rows, earlier_force):
    devices = arrived.shape[0]
    clusters, _, nodes = node_rows.shape
    batch = min(BATCH, devices * SHARE)
    sources = batch // SHARE
    width = GROUP // SHARE * LANES
    last = part == PARTS - 1
    force_shape = (3, clusters, nodes) if last else (clusters, 8, nodes)
    room = batch * width + clusters * CHUNK + 3 * CHUNK + 2 * WINDOW
    extra = () if earlier_force is None else (earlier_force,)
    pairs = devices * SHARE * width // 4
    return pl.pallas_call(
        functools.partial(couple_kernel, part),
        grid=(devices * SHARE // batch,),
        out_shape=(
            jax.ShapeDtypeStruct((devices, 3 * GROUP, LANES), F32),
            jax.ShapeDtypeStruct(force_shape, F32),
        ),
        in_specs=[
            pl.BlockSpec((sources, GROUP, LANES), lambda i: (i, 6, 0)),
            pl.BlockSpec((sources, 6 * GROUP, LANES), lambda i: (i, 0, 0)),
            vmem(),
            vmem(),
            vmem(),
        ]
        + [vmem() for _ in extra],
        out_specs=(
            pl.BlockSpec((sources, 3 * GROUP, LANES), lambda i: (i, 0, 0)),
            pl.BlockSpec(force_shape, lambda i: (0, 0, 0)),
        ),
        scratch_shapes=[
            pltpu.VMEM((batch, width), F32),
            pltpu.VMEM((batch, LANES), F32),
            pltpu.VMEM((batch, LANES), F32),
            pltpu.VMEM((GROUP // SHARE, 32 * GROUP, LANES), F32),
            pltpu.VMEM((room, LANES), F32),
            pltpu.VMEM((CHUNK, nodes), F32),
            pltpu.VMEM((CHUNK, nodes), F32),
            pltpu.VMEM((8, batch), jnp.int32),
            pltpu.VMEM((clusters, LANES), jnp.int32),
            pltpu.SMEM((8, batch), jnp.int32),
            pltpu.SMEM((clusters, LANES), jnp.int32),
            pltpu.SMEM((room // CHUNK + 4,), jnp.int32),
            pltpu.VMEM((clusters, 8, nodes), F32),
            pltpu.SemaphoreType.DMA((2,)),
        ],
        compiler_params=pltpu.CompilerParams(vmem_limit_bytes=40 * 1024 * 1024),
        cost_estimate=pl.CostEstimate(
            flops=pairs * nodes * 80, bytes_accessed=arrived.size * 6, transcendentals=pairs * nodes
        ),
        name=f"couple_{part}",
    )(id_source, arrived, table, node_rows, coeff_rows, *extra)


def exchange(x):
    return lax.all_to_all(x, AXES, split_axis=0, concat_axis=0, tiled=True)


def on_device(point_coords, fluid_force, tile_clusters, pu_level, node_coords, node_disp, inverse):
    highest = lax.Precision.HIGHEST
    devices = lax.axis_size(AXES)
    slot_total = devices * CAP
    tile_total, kslots = tile_clusters.shape
    pair_total = tile_total * kslots
    local_count, _, node_count = node_coords.shape
    width = point_coords.shape[2]
    points = jnp.transpose(point_coords, (1, 0, 2))

    outgoing, loads, pair_of = pl.pallas_call(
        functools.partial(first_pack_kernel, local_count, pair_total == slot_total),
        out_shape=(
            jax.ShapeDtypeStruct((devices, 7 * GROUP, LANES), F32),
            jax.ShapeDtypeStruct((3, pair_total, width), F32),
            jax.ShapeDtypeStruct((slot_total,), jnp.int32),
        ),
        in_specs=[smem(), vmem(), vmem(), vmem()],
        out_specs=(vmem(), vmem(), smem()),
        scratch_shapes=[pltpu.SMEM((devices,), jnp.int32)],
        name="pack_0",
    )(tile_clusters.reshape(-1), points, jnp.transpose(fluid_force, (1, 0, 2)), pu_level)
    arrived = exchange(outgoing)

    coeffs = jnp.einsum("cin,cnm->cim", node_disp, inverse, precision=highest) * (1.0 / 256.0)
    high, low = outer_split(coeffs, 2)
    gap5 = jnp.zeros((local_count, 5, node_count), F32)
    coeff_rows = jnp.concatenate((high, gap5, low, gap5), axis=1).astype(BF16)
    least = jnp.min(node_coords, axis=2)
    most = jnp.max(node_coords, axis=2)
    centre = 0.5 * (least + most)
    nodes = node_coords - centre[:, :, None]
    near = [-32.0 * piece for piece in outer_split(nodes, 3)]
    square = [16.0 * p for p in outer_split(jnp.sum(nodes * nodes, axis=1, keepdims=True), 3)]
    sixteen = jnp.full((local_count, 3, node_count), 16.0, F32)
    rows = [near[0]] * 3 + [near[1]] * 2 + [near[2], sixteen] + square
    rows.append(jnp.zeros((local_count, 8, node_count), F32))
    node_rows = jnp.concatenate(rows, axis=1).astype(BF16)
    table = jnp.concatenate((least, most, centre), axis=1)
    table = jnp.concatenate(outer_split(table, 3), axis=0).astype(BF16)
    table = jnp.pad(table, ((0, LANES - table.shape[0]), (0, LANES - table.shape[1])))

    id_source = arrived
    force = None
    backs = []
    for part in range(PARTS):
        following = None
        if part + 1 < PARTS:
            packed = pl.pallas_call(
                functools.partial(next_pack_kernel, part + 1),
                out_shape=jax.ShapeDtypeStruct((devices, 6 * GROUP, LANES), F32),
                in_specs=[smem(), vmem(), vmem()],
                out_specs=vmem(),
                name=f"pack_{part + 1}",
            )(pair_of, points, loads)
            packed, arrived, table, node_rows, coeff_rows = lax.optimization_barrier(
                (packed, arrived, table, node_rows, coeff_rows)
            )
            if part == 0:
                id_source = arrived
            following = exchange(packed)
        values, force = couple(part, id_source, arrived, table, node_rows, coeff_rows, force)
        backs.append(exchange(values))
        arrived = following

    point_disp = pl.pallas_call(
        unpack_kernel,
        out_shape=jax.ShapeDtypeStruct((3, tile_total, width), F32),
        in_specs=[smem()] + [vmem()] * (PARTS + 1),
        out_specs=vmem(),
        scratch_shapes=[pltpu.VMEM((3, pair_total + 8, width), F32)],
        name="unpack",
    )(pair_of, *backs, pu_level)
    return jnp.transpose(point_disp, (1, 0, 2)), jnp.transpose(force, (1, 0, 2))


def solution(mesh):
    placed = (
        P(AXES, None, None),
        P(AXES, None, None),
        P(AXES, None),
        P(AXES, None, None),
        P(AXES, None, None),
        P(AXES, None, None),
        P(AXES, None, None),
    )
    return jax.shard_map(
        on_device,
        mesh=mesh,
        in_specs=placed,
        out_specs=(P(AXES, None, None), P(AXES, None, None)),
        check_vma=False,
    )
```

time: 683 us -> 127 us (0.19)
  matrix products: 397 us -> 11.7 us
  other arithmetic: 136 us -> 2.45 us
  local copies, waits for them, and re-layouts: 87 us -> 2.68 us
  Pallas kernels: 0 us -> 65.2 us
  waiting for transfers between devices: 41.7 us -> 4.65 us
  blocking collectives: 0 us -> 21.4 us
    dot_general x66 -> x1, matrix products: 397 us -> 11.7 us  [on_device(): jnp.einsum('cin,cnm->cim', node_disp, inverse, precision=highest)]
    reduce_sum x35 -> x1, other arithmetic: 129 us -> 0.98 us  [on_device(): jnp.sum(nodes * nodes, axis=1, keepdims=True)]
    pallas_call x0 -> x5, Pallas kernels: none -> 65.2 us  [the longest x2 52.4 us: couple(): pl.pallas_call(functools.partial(couple_kernel, part), grid=(devices * SH...]
    gather x65 -> x0, local copies, waits for them, and re-layouts: 38.9 us -> none  [the longest x32 18.8 us: per_group(): jnp.take(node_coords, slot_ids, axis=0)]
    all_to_all x3, waiting for transfers between devices: 41.7 us -> 4.65 us  [exchange(): return lax.all_to_all(x, AXES, split_axis=0, concat_axis=0, tiled=True)]
    all_to_all x0 -> x1, blocking collectives: none -> 21.4 us  [exchange(): return lax.all_to_all(x, AXES, split_axis=0, concat_axis=0, tiled=True)]
    dynamic_update_slice x32 -> x0, local copies, waits for them, and re-layouts: 20.1 us -> none  [on_device(): lax.map(per_group, (slot_ids, arrived.reshape(-1, group_size, 6, tile_wid...]
    scatter x1 -> x0, local copies, waits for them, and re-layouts: 18.6 us -> none  [on_device(): jnp.zeros((slot_total, 6, tile_width), jnp.float32).at[slot_of].set(packed)]
  transfers between devices with their start and end apart: 3 -> 3, of which waited for: 2 -> 1; matrix products, arithmetic and copies ran while one was open for 6% -> 12% of each run, Pallas kernels for 0% -> 44%
where the time goes in v2:
time: 127 us; the launch traced here: 126 us
  Pallas kernels  65.2 us (51%)
  blocking collectives  21.4 us (17%)
  starting transfers between devices  17.4 us (14%)
  matrix products  11.7 us (9%)
  waiting for transfers between devices  4.65 us (4%)
  local copies, waits for them, and re-layouts  2.68 us (2%)
  other arithmetic  2.45 us (2%)
    pallas_call x2, Pallas kernels, couple(): pl.pallas_call(functools.partial(couple_kernel, part), grid=(devices * SH...  52.4 us
    all_to_all x1, blocking collectives, exchange(): return lax.all_to_all(x, AXES, split_axis=0, concat_axis=0, tiled=True)  21.4 us
    all_to_all x3, starting transfers between devices, exchange(): return lax.all_to_all(x, AXES, split_axis=0, concat_axis=0, tiled=True)  17.4 us
    dot_general x1, matrix products, on_device(): jnp.einsum('cin,cnm->cim', node_disp, inverse, precision=highest)  11.7 us
    pallas_call x1, Pallas kernels, on_device(): pl.pallas_call(functools.partial(first_pack_kernel, local_count, pair_tot...  6.03 us
    all_to_all x3, waiting for transfers between devices, exchange(): return lax.all_to_all(x, AXES, split_axis=0, concat_axis=0, tiled=True)  4.65 us
    pallas_call x1, Pallas kernels, on_device(): pl.pallas_call(unpack_kernel, out_shape=jax.ShapeDtypeStruct((3, tile_tot...  3.59 us
    pallas_call x1, Pallas kernels, on_device(): pl.pallas_call(functools.partial(next_pack_kernel, part + 1), out_shape=j...  3.24 us
  transfers between devices with their start and end apart: 3, of which 1 were waited for; matrix products, arithmetic and copies ran while one was open for 12% of the time, Pallas kernels for 44%

profile of v2, /device:TPU:0, one launch (start us, length us, event | category | flops | bytes accessed | tf_op | source)
XLA Modules:
  0.0 126.3 jit_solution(7101534966219594243)
XLA Ops:
  0.6 0.8 copy.19
  1.4 0.7 reshape.57.ids
  2.0 6.0 %pack_0.1 = (f32[32,56,128]{2,1,0:T(8,128)}, f32[3,256,256]{2,1,0:T(8,128)}, s32[256]{0:T(256)}) custom-call(s32[256]{0:T(256)} %reshape.57.ids, f32[3,32,256]{2,1,0:T(8,128)} %bitcast.5, f32[3,32,256]{2,1,0:T(8,128)} %bitcast.7, s32[32,8,256]{2,1,0:T(8,128)} %refs_2_.1), custom_call_target="tpu_custom_call" | custom-call | tf_op jit(solution)/shard_map/pack_0/pallas_call | solution.py:483
  8.1 7.3 %all-to-all-start = ((f32[32,56,128]{2,1,0:T(8,128)}), f32[32,56,128]{2,1,0:T(8,128)S(1)}, u32[]{:S(2)}, u32[]{:S(2)}) async-start(f32[32,56,128]{2,1,0:T(8,128)} %get-tuple-element.16), calls=%async_computation | async-start | bytes 1835008 | tf_op jit(solution)/shard_map/all_to_all | solution.py:470
  15.4 1.0 fusion.15
  16.4 0.1 pad_maximum_fusion.2
  16.5 0.1 copy.20
  16.7 3.2 %pack_1.1 = f32[32,48,128]{2,1,0:T(8,128)} custom-call(s32[256]{0:T(256)} %get-tuple-element.14.pair_of, f32[3,32,256]{2,1,0:T(8,128)} %bitcast.6, f32[3,256,256]{2,1,0:T(8,128)} %get-tuple-element.15.loads), custom_call_target="tpu_custom_call" | custom-call | tf_op jit(solution)/shard_map/pack_1/pallas_call | solution.py:521
  19.9 1.0 multiply_reduce_fusion
  20.9 0.1 fusion.12
  21.0 0.1 fusion.4
  21.2 1.1 concatenate.17.refs_3_
  22.3 11.7 %reduce-precision_convert_fusion = (bf16[16,3,512]{2,1,0:T(4,128)(2,1)S(1)}, bf16[16,3,512]{2,1,0:T(4,128)(2,1)S(1)}) fusion(f32[16,512,512]{2,1,0:T(8,128)} %param.13, f32[16,3,512]{2,0,1:T(8,128)} %param.12), kind=kOutput, calls=%fused_computation.3 | convolution fusion | flops 151142400 | bytes 16973824 | tf_op jit(solution)/shard_map/cin,cnm->cim/dot_general | solution.py:497
  34.0 0.2 pad_maximum_fusion.refs_4_
  34.2 4.6 %all-to-all-done.refs_0_.refs_1_ = f32[32,56,128]{2,1,0:T(8,128)S(1)} async-done(((f32[32,56,128]{2,1,0:T(8,128)}), f32[32,56,128]{2,1,0:T(8,128)S(1)}, u32[]{:S(2)}, u32[]{:S(2)}) %all-to-all-start) | async-done | bytes 917536 | tf_op jit(solution)/shard_map/all_to_all | solution.py:470
  38.8 3.6 %all-to-all-start.2 = ((f32[32,48,128]{2,1,0:T(8,128)}), f32[32,48,128]{2,1,0:T(8,128)S(1)}, u32[]{:S(2)}, u32[]{:S(2)}) async-start(f32[32,48,128]{2,1,0:T(8,128)} %pack_1.1), calls=%async_computation.2 | async-start | bytes 1572864 | tf_op jit(solution)/shard_map/all_to_all | solution.py:470
  42.4 26.2 %couple_0.1 = (f32[32,24,128]{2,1,0:T(8,128)}, f32[16,8,512]{2,1,0:T(8,128)S(1)}) custom-call(f32[32,56,128]{2,1,0:T(8,128)S(1)} %all-to-all-done.refs_0_.refs_1_, f32[32,56,128]{2,1,0:T(8,128)S(1)} %all-to-all-done.refs_0_.refs_1_, bf16[128,128]{1,0:T(8,128)(2,1)S(1)} %pad.4.refs_2_, bf16[16,32,512]{2,1,0:T(8,128)(2,1)S(1)} %concatenate.17.refs_3_, ...), custom_call_target="tpu_custom_call" | custom-call | flops 335544320 | bytes 1376256 | tf_op jit(solution)/shard_map/couple_0/pallas_call | solution.py:426
  68.7 0.0 all-to-all-done.2.refs_1_
  68.7 6.4 %all-to-all-start.1 = ((f32[32,24,128]{2,1,0:T(8,128)}), f32[32,24,128]{2,1,0:T(8,128)}, u32[]{:S(2)}, u32[]{:S(2)}) async-start(f32[32,24,128]{2,1,0:T(8,128)} %get-tuple-element.21), calls=%async_computation.1 | async-start | bytes 786432 | tf_op jit(solution)/shard_map/all_to_all | solution.py:470
  75.1 26.1 %couple_1.1 = (f32[32,24,128]{2,1,0:T(8,128)S(1)}, f32[3,16,512]{2,1,0:T(8,128)}) custom-call(f32[32,56,128]{2,1,0:T(8,128)S(1)} %all-to-all-done.refs_0_.refs_1_, f32[32,48,128]{2,1,0:T(8,128)S(1)} %all-to-all-done.2.refs_1_, bf16[128,128]{1,0:T(8,128)(2,1)S(1)} %pad.4.refs_2_, bf16[16,32,512]{2,1,0:T(8,128)(2,1)S(1)} %concatenate.17.refs_3_, ...), custom_call_target="tpu_custom_call" | custom-call | flops 335544320 | bytes 1179648 | tf_op jit(solution)/shard_map/couple_1/pallas_call | solution.py:426
  101.3 0.0 all-to-all-done.1.refs_0_
  101.3 21.4 %all_to_all.20.refs_1_ = f32[32,24,128]{2,1,0:T(8,128)} all-to-all(f32[32,24,128]{2,1,0:T(8,128)S(1)} %get-tuple-element.24), channel_id=1, replica_groups=mesh['row'=4,'col'=8] {'row','col'}, dimensions={0} | all-to-all | bytes 786432 | tf_op jit(solution)/shard_map/all_to_all | solution.py:470
  122.7 3.6 %unpack.1 = f32[3,32,256]{2,1,0:T(8,128)} custom-call(s32[256]{0:T(256)} %get-tuple-element.14.pair_of, f32[32,24,128]{2,1,0:T(8,128)} %all-to-all-done.1.refs_0_, f32[32,24,128]{2,1,0:T(8,128)} %all_to_all.20.refs_1_, s32[32,8,256]{2,1,0:T(8,128)} %refs_2_.1), custom_call_target="tpu_custom_call" | custom-call | tf_op jit(solution)/shard_map/unpack/pallas_call | solution.py:538
  (6 shorter events, 0.1 us)
Async XLA Ops:
  8.1 30.7 %all-to-all-start = ((f32[32,56,128]{2,1,0:T(8,128)}), f32[32,56,128]{2,1,0:T(8,128)S(1)}, u32[]{:S(2)}, u32[]{:S(2)}) async-start(f32[32,56,128]{2,1,0:T(8,128)} %get-tuple-element.16), calls=%async_computation | async-start | bytes 1835008 | tf_op jit(solution)/shard_map/all_to_all | solution.py:470
  38.8 29.9 %all-to-all-start.2 = ((f32[32,48,128]{2,1,0:T(8,128)}), f32[32,48,128]{2,1,0:T(8,128)S(1)}, u32[]{:S(2)}, u32[]{:S(2)}) async-start(f32[32,48,128]{2,1,0:T(8,128)} %pack_1.1), calls=%async_computation.2 | async-start | bytes 1572864 | tf_op jit(solution)/shard_map/all_to_all | solution.py:470
  68.7 32.6 %all-to-all-start.1 = ((f32[32,24,128]{2,1,0:T(8,128)}), f32[32,24,128]{2,1,0:T(8,128)}, u32[]{:S(2)}, u32[]{:S(2)}) async-start(f32[32,24,128]{2,1,0:T(8,128)} %get-tuple-element.21), calls=%async_computation.1 | async-start | bytes 786432 | tf_op jit(solution)/shard_map/all_to_all | solution.py:470

commit v3 on v2

--- a/solution.py
+++ b/solution.py
@@ -13,6 +13,7 @@
 GROUP = 8
 BATCH = 128
 CHUNK = 256
+TEAM = 4
 WINDOW = 96
 LANES = 128
 AXES = ("row", "col")
@@ -144,6 +145,7 @@
     id_tiles, arrived, table, node_rows, coeff_rows = refs[:5]
     del refs[:5]
     earlier_force = None if first else refs.pop(0)
+    id_row = id_tiles.shape[1] - CAP + part * SHARE
     values, node_force = refs[:2]
     (
         rank,
@@ -151,6 +153,7 @@
         boxes,
         rows,
         packed,
+        found_rows,
         even,
         odd,
         slot_plan_v,
@@ -184,7 +187,7 @@
     def _(g):
         id_rows[group_rows(g), :] = jnp.concatenate(
             [
-                id_tiles[g * per_group + i, part * SHARE : (part + 1) * SHARE, :]
+                id_tiles[g * per_group + i, id_row : id_row + SHARE, :]
                 for i in range(per_group)
             ],
             axis=0,
@@ -260,15 +263,18 @@
     def _(j):
         packed[chunk_rows(j), :] = jnp.zeros((CHUNK, LANES), F32)
 
+    for extra in range(2):
+        found_rows[chunk_rows(total_chunks + extra), 0:16] = jnp.zeros((CHUNK, 16), F32)
+
     for extra in range(3):
         cluster_of[total_chunks + extra] = 0
 
     target = iota((WINDOW, 1), 0).astype(F32)
 
-    def places_of(g):
+    def places_of(team):
         places = []
-        for i in range(GROUP):
-            slot = g * GROUP + i
+        for i in range(TEAM * GROUP):
+            slot = team * (TEAM * GROUP) + i
             start = slot_plan[0, slot]
             base = (start // 8) * 8
             lead = start - base
@@ -286,11 +292,11 @@
     def window_of(place, block):
         return pl.ds(pl.multiple_of(place[1] + block * WINDOW, 8), WINDOW)
 
-    @pl.loop(0, groups)
-    def _(g):
-        for i in range(per_group):
-            d = g * per_group + i
-            box = slot_tiles(boxes[group_rows(g), :], i)
+    @pl.loop(0, groups // TEAM)
+    def _(team):
+        for i in range(TEAM * per_group):
+            d = team * (TEAM * per_group) + i
+            box = slot_tiles(boxes[group_rows(team * TEAM + i // per_group), :], i % per_group)
             x = [
                 arrived[d, c * GROUP : (c + 1) * GROUP, :] - box[:, 6 + c : 7 + c] for c in range(3)
             ]
@@ -303,7 +309,7 @@
             column += [jnp.zeros_like(x[0])] * 2
             for n, tile in enumerate(column):
                 rows[i, n * GROUP : (n + 1) * GROUP, :] = tile
-        places, most = places_of(g)
+        places, most = places_of(team)
 
         def gathered(i, block):
             source = rows.at[i // SHARE]
@@ -317,13 +323,13 @@
                 preferred_element_type=F32,
             )
 
-        moved = [gathered(i, 0) for i in range(GROUP)]
-        for i in range(GROUP):
+        moved = [gathered(i, 0) for i in range(TEAM * GROUP)]
+        for i in range(TEAM * GROUP):
             packed[window_of(places[i], 0), 0:32] += moved[i]
 
         @pl.when(most > 1)
         def _():
-            for i in range(GROUP):
+            for i in range(TEAM * GROUP):
 
                 @pl.loop(1, places[i][3])
                 def _(block):
@@ -345,7 +351,7 @@
         high = kernel.astype(BF16)
         low = (kernel - high.astype(F32)).astype(BF16)
         loads = jnp.transpose(packed[chunk_rows(j), :])[24:32].astype(BF16)
-        packed[chunk_rows(j), 0:16] = lax.dot_general(
+        found_rows[chunk_rows(j), 0:16] = lax.dot_general(
             high, coeff_rows[c], NT, preferred_element_type=F32
         ) + lax.dot_general(low, coeff_rows[c], NT, preferred_element_type=F32)
         force_sum[c] += jnp.dot(loads, high, preferred_element_type=F32) + jnp.dot(
@@ -361,32 +367,32 @@
         distances(2 * j + 2, even)
         contract(2 * j + 1, odd)
 
-    @pl.loop(0, groups)
-    def _(g):
-        places, most = places_of(g)
+    @pl.loop(0, groups // TEAM)
+    def _(team):
+        places, most = places_of(team)
 
         def spread(i, block):
-            rows_t = jnp.transpose(packed[window_of(places[i], block), :])
+            rows_t = jnp.transpose(found_rows[window_of(places[i], block), :])
             high, middle, low = split3(rows_t[0:8] + rows_t[8:16])
             stacked = jnp.concatenate([high, middle, low], axis=0).astype(BF16)
             moved = jnp.dot(stacked, selection(places[i], block), preferred_element_type=F32)
             return moved[0:8] + moved[8:16] + moved[16:24]
 
         def pieces_of(i, found):
-            d = g * per_group + i // SHARE
+            d = team * (TEAM * per_group) + i // SHARE
             for c in range(3):
                 for h in range(halves):
                     row = c * GROUP + h * SHARE + i % SHARE
                     yield d, row, found[c : c + 1, h * LANES : (h + 1) * LANES]
 
-        spreads = [spread(i, 0) for i in range(GROUP)]
-        for i in range(GROUP):
+        spreads = [spread(i, 0) for i in range(TEAM * GROUP)]
+        for i in range(TEAM * GROUP):
             for d, row, piece in pieces_of(i, spreads[i]):
                 values[d, row : row + 1, :] = piece
 
         @pl.when(most > 1)
         def _():
-            for i in range(GROUP):
+            for i in range(TEAM * GROUP):
 
                 @pl.loop(1, places[i][3])
                 def _(block):
@@ -419,34 +425,36 @@
     sources = batch // SHARE
     width = GROUP // SHARE * LANES
     last = part == PARTS - 1
+    steps = devices * SHARE // batch
     force_shape = (3, clusters, nodes) if last else (clusters, 8, nodes)
     room = batch * width + clusters * CHUNK + 3 * CHUNK + 2 * WINDOW
     extra = () if earlier_force is None else (earlier_force,)
     pairs = devices * SHARE * width // 4
     return pl.pallas_call(
         functools.partial(couple_kernel, part),
-        grid=(devices * SHARE // batch,),
+        grid=(steps,),
         out_shape=(
             jax.ShapeDtypeStruct((devices, 3 * GROUP, LANES), F32),
             jax.ShapeDtypeStruct(force_shape, F32),
         ),
         in_specs=[
-            pl.BlockSpec((sources, GROUP, LANES), lambda i: (i, 6, 0)),
-            pl.BlockSpec((sources, 6 * GROUP, LANES), lambda i: (i, 0, 0)),
+            vmem() if steps == 1 else pl.BlockSpec((sources, GROUP, LANES), lambda i: (i, 6, 0)),
+            vmem() if steps == 1 else pl.BlockSpec((sources, 6 * GROUP, LANES), lambda i: (i, 0, 0)),
             vmem(),
             vmem(),
             vmem(),
         ]
         + [vmem() for _ in extra],
         out_specs=(
-            pl.BlockSpec((sources, 3 * GROUP, LANES), lambda i: (i, 0, 0)),
-            pl.BlockSpec(force_shape, lambda i: (0, 0, 0)),
+            vmem() if steps == 1 else pl.BlockSpec((sources, 3 * GROUP, LANES), lambda i: (i, 0, 0)),
+            vmem() if steps == 1 else pl.BlockSpec(force_shape, lambda i: (0, 0, 0)),
         ),
         scratch_shapes=[
             pltpu.VMEM((batch, width), F32),
             pltpu.VMEM((batch, LANES), F32),
             pltpu.VMEM((batch, LANES), F32),
-            pltpu.VMEM((GROUP // SHARE, 32 * GROUP, LANES), F32),
+            pltpu.VMEM((TEAM * GROUP // SHARE, 32 * GROUP, LANES), F32),
+            pltpu.VMEM((room, LANES), F32),
             pltpu.VMEM((room, LANES), F32),
             pltpu.VMEM((CHUNK, nodes), F32),
             pltpu.VMEM((CHUNK, nodes), F32),
@@ -458,7 +466,7 @@
             pltpu.VMEM((clusters, 8, nodes), F32),
             pltpu.SemaphoreType.DMA((2,)),
         ],
-        compiler_params=pltpu.CompilerParams(vmem_limit_bytes=40 * 1024 * 1024),
+        compiler_params=pltpu.CompilerParams(vmem_limit_bytes=52 * 1024 * 1024),
         cost_estimate=pl.CostEstimate(
             flops=pairs * nodes * 80, bytes_accessed=arrived.size * 6, transcendentals=pairs * nodes
         ),

time: 127 us -> 119 us (0.937)
  Pallas kernels: 65.2 us -> 60.9 us
  starting transfers between devices: 17.4 us -> 15.6 us
  blocking collectives: 21.4 us -> 19.7 us
    pallas_call x2, Pallas kernels: 52.4 us -> 48 us  [couple(): pl.pallas_call(functools.partial(couple_kernel, part), grid=(steps,), out...]
    all_to_all x3, starting transfers between devices: 17.4 us -> 15.6 us  [exchange(): return lax.all_to_all(x, AXES, split_axis=0, concat_axis=0, tiled=True)]
    all_to_all x1, blocking collectives: 21.4 us -> 19.7 us  [exchange(): return lax.all_to_all(x, AXES, split_axis=0, concat_axis=0, tiled=True)]
  transfers between devices with their start and end apart: 3 -> 3, of which waited for: 1 -> 1; matrix products, arithmetic and copies ran while one was open for 12% -> 13% of each run, Pallas kernels for 44% -> 43%
where the time goes in v3:
time: 119 us; the launch traced here: 118 us
  Pallas kernels  60.9 us (51%)
  blocking collectives  19.7 us (17%)
  starting transfers between devices  15.6 us (13%)
  matrix products  11.7 us (10%)
  waiting for transfers between devices  4.62 us (4%)
  local copies, waits for them, and re-layouts  2.69 us (2%)
  other arithmetic  2.45 us (2%)
    pallas_call x2, Pallas kernels, couple(): pl.pallas_call(functools.partial(couple_kernel, part), grid=(steps,), out...  48 us
    all_to_all x1, blocking collectives, exchange(): return lax.all_to_all(x, AXES, split_axis=0, concat_axis=0, tiled=True)  19.7 us
    all_to_all x3, starting transfers between devices, exchange(): return lax.all_to_all(x, AXES, split_axis=0, concat_axis=0, tiled=True)  15.6 us
    dot_general x1, matrix products, on_device(): jnp.einsum('cin,cnm->cim', node_disp, inverse, precision=highest)  11.7 us
    pallas_call x1, Pallas kernels, on_device(): pl.pallas_call(functools.partial(first_pack_kernel, local_count, pair_tot...  5.99 us
    all_to_all x3, waiting for transfers between devices, exchange(): return lax.all_to_all(x, AXES, split_axis=0, concat_axis=0, tiled=True)  4.62 us
    pallas_call x1, Pallas kernels, on_device(): pl.pallas_call(unpack_kernel, out_shape=jax.ShapeDtypeStruct((3, tile_tot...  3.59 us
    pallas_call x1, Pallas kernels, on_device(): pl.pallas_call(functools.partial(next_pack_kernel, part + 1), out_shape=j...  3.28 us
  transfers between devices with their start and end apart: 3, of which 1 were waited for; matrix products, arithmetic and copies ran while one was open for 13% of the time, Pallas kernels for 43%

profile of v3, /device:TPU:0, one launch (start us, length us, event | category | flops | bytes accessed | tf_op | source)
XLA Modules:
  0.0 118.4 jit_solution(2259189230516714301)
XLA Ops:
  0.6 0.8 copy.19
  1.4 0.7 reshape.57.ids
  2.0 6.0 %pack_0.1 = (f32[32,56,128]{2,1,0:T(8,128)}, f32[3,256,256]{2,1,0:T(8,128)}, s32[256]{0:T(256)}) custom-call(s32[256]{0:T(256)} %reshape.57.ids, f32[3,32,256]{2,1,0:T(8,128)} %bitcast.5, f32[3,32,256]{2,1,0:T(8,128)} %bitcast.7, s32[32,8,256]{2,1,0:T(8,128)} %refs_2_.1), custom_call_target="tpu_custom_call" | custom-call | tf_op jit(solution)/shard_map/pack_0/pallas_call | solution.py:491
  8.0 7.3 %all-to-all-start = ((f32[32,56,128]{2,1,0:T(8,128)}), f32[32,56,128]{2,1,0:T(8,128)S(1)}, u32[]{:S(2)}, u32[]{:S(2)}) async-start(f32[32,56,128]{2,1,0:T(8,128)} %get-tuple-element.16), calls=%async_computation | async-start | bytes 1835008 | tf_op jit(solution)/shard_map/all_to_all | solution.py:478
  15.4 1.0 fusion.15
  16.4 0.1 pad_maximum_fusion.2
  16.5 0.1 copy.20
  16.6 3.3 %pack_1.1 = f32[32,48,128]{2,1,0:T(8,128)} custom-call(s32[256]{0:T(256)} %get-tuple-element.14.pair_of, f32[3,32,256]{2,1,0:T(8,128)} %bitcast.6, f32[3,256,256]{2,1,0:T(8,128)} %get-tuple-element.15.loads), custom_call_target="tpu_custom_call" | custom-call | tf_op jit(solution)/shard_map/pack_1/pallas_call | solution.py:529
  19.9 1.0 multiply_reduce_fusion
  20.9 0.1 fusion.12
  21.0 0.1 fusion.4
  21.2 1.1 concatenate.17.refs_3_
  22.3 11.7 %reduce-precision_convert_fusion = (bf16[16,3,512]{2,1,0:T(4,128)(2,1)S(1)}, bf16[16,3,512]{2,1,0:T(4,128)(2,1)S(1)}) fusion(f32[16,512,512]{2,1,0:T(8,128)} %param.13, f32[16,3,512]{2,0,1:T(8,128)} %param.12), kind=kOutput, calls=%fused_computation.3 | convolution fusion | flops 151142400 | bytes 16973824 | tf_op jit(solution)/shard_map/cin,cnm->cim/dot_general | solution.py:505
  34.0 0.2 pad_maximum_fusion.refs_4_
  34.2 4.6 %all-to-all-done.refs_0_.refs_1_ = f32[32,56,128]{2,1,0:T(8,128)S(1)} async-done(((f32[32,56,128]{2,1,0:T(8,128)}), f32[32,56,128]{2,1,0:T(8,128)S(1)}, u32[]{:S(2)}, u32[]{:S(2)}) %all-to-all-start) | async-done | bytes 917536 | tf_op jit(solution)/shard_map/all_to_all | solution.py:478
  38.8 0.0 copy-start.1
  38.8 3.6 %all-to-all-start.2 = ((f32[32,48,128]{2,1,0:T(8,128)}), f32[32,48,128]{2,1,0:T(8,128)S(1)}, u32[]{:S(2)}, u32[]{:S(2)}) async-start(f32[32,48,128]{2,1,0:T(8,128)} %pack_1.1), calls=%async_computation.2 | async-start | bytes 1572864 | tf_op jit(solution)/shard_map/all_to_all | solution.py:478
  42.4 0.0 copy-done.1
  42.4 24.5 %couple_0.1 = (f32[32,24,128]{2,1,0:T(8,128)}, f32[16,8,512]{2,1,0:T(8,128)S(1)}) custom-call(f32[32,56,128]{2,1,0:T(8,128)} %copy-done.1, f32[32,56,128]{2,1,0:T(8,128)} %copy-done.1, bf16[128,128]{1,0:T(8,128)(2,1)S(1)} %pad.4.refs_2_, bf16[16,32,512]{2,1,0:T(8,128)(2,1)S(1)} %concatenate.17.refs_3_, bf16[16,16,512]{2,1,0:T(8,128)(2,1)S(1)} %pad_maximum_fusion.refs_4_), custom_call_target="tpu_custom_call" | custom-call | flops 335544320 | bytes 1376256 | tf_op jit(solution)/shard_map/couple_0/pallas_call | solution.py:433
  66.9 0.0 all-to-all-done.2.refs_1_
  66.9 0.0 copy-start.2
  66.9 4.7 %all-to-all-start.1 = ((f32[32,24,128]{2,1,0:T(8,128)}), f32[32,24,128]{2,1,0:T(8,128)S(1)}, u32[]{:S(2)}, u32[]{:S(2)}) async-start(f32[32,24,128]{2,1,0:T(8,128)} %get-tuple-element.21), calls=%async_computation.1 | async-start | bytes 786432 | tf_op jit(solution)/shard_map/all_to_all | solution.py:478
  71.6 0.0 copy-done.2
  71.6 23.5 %couple_1.1 = (f32[32,24,128]{2,1,0:T(8,128)S(1)}, f32[3,16,512]{2,1,0:T(8,128)}) custom-call(f32[32,56,128]{2,1,0:T(8,128)} %copy-done.1, f32[32,48,128]{2,1,0:T(8,128)} %copy-done.2, bf16[128,128]{1,0:T(8,128)(2,1)S(1)} %pad.4.refs_2_, bf16[16,32,512]{2,1,0:T(8,128)(2,1)S(1)} %concatenate.17.refs_3_, bf16[16,16,512]{2,1,0:T(8,128)(2,1)S(1)} %pad_maximum_fusion.refs_4_, ...), custom_call_target="tpu_custom_call" | custom-call | flops 335544320 | bytes 1179648 | tf_op jit(solution)/shard_map/couple_1/pallas_call | solution.py:433
  95.1 0.0 all-to-all-done.1.refs_0_
  95.1 0.0 copy-start
  95.1 19.7 %all_to_all.20.refs_1_ = f32[32,24,128]{2,1,0:T(8,128)} all-to-all(f32[32,24,128]{2,1,0:T(8,128)S(1)} %get-tuple-element.24), channel_id=1, replica_groups=mesh['row'=4,'col'=8] {'row','col'}, dimensions={0} | all-to-all | bytes 786432 | tf_op jit(solution)/shard_map/all_to_all | solution.py:478
  114.8 0.0 copy-done
  114.9 3.6 %unpack.1 = f32[3,32,256]{2,1,0:T(8,128)} custom-call(s32[256]{0:T(256)} %get-tuple-element.14.pair_of, f32[32,24,128]{2,1,0:T(8,128)} %copy-done, f32[32,24,128]{2,1,0:T(8,128)} %all_to_all.20.refs_1_, s32[32,8,256]{2,1,0:T(8,128)} %refs_2_.1), custom_call_target="tpu_custom_call" | custom-call | tf_op jit(solution)/shard_map/unpack/pallas_call | solution.py:546
  (6 shorter events, 0.1 us)
Async XLA Ops:
  8.0 30.7 %all-to-all-start = ((f32[32,56,128]{2,1,0:T(8,128)}), f32[32,56,128]{2,1,0:T(8,128)S(1)}, u32[]{:S(2)}, u32[]{:S(2)}) async-start(f32[32,56,128]{2,1,0:T(8,128)} %get-tuple-element.16), calls=%async_computation | async-start | bytes 1835008 | tf_op jit(solution)/shard_map/all_to_all | solution.py:478
  38.8 3.6 %copy-start.1 = (f32[32,56,128]{2,1,0:T(8,128)}, f32[32,56,128]{2,1,0:T(8,128)S(1)}, u32[]{:S(2)}) copy-start(f32[32,56,128]{2,1,0:T(8,128)S(1)} %all-to-all-done.refs_0_.refs_1_) | copy-start | bytes 2752516
  38.8 28.1 %all-to-all-start.2 = ((f32[32,48,128]{2,1,0:T(8,128)}), f32[32,48,128]{2,1,0:T(8,128)S(1)}, u32[]{:S(2)}, u32[]{:S(2)}) async-start(f32[32,48,128]{2,1,0:T(8,128)} %pack_1.1), calls=%async_computation.2 | async-start | bytes 1572864 | tf_op jit(solution)/shard_map/all_to_all | solution.py:478
  66.9 4.7 %copy-start.2 = (f32[32,48,128]{2,1,0:T(8,128)}, f32[32,48,128]{2,1,0:T(8,128)S(1)}, u32[]{:S(2)}) copy-start(f32[32,48,128]{2,1,0:T(8,128)S(1)} %all-to-all-done.2.refs_1_) | copy-start | bytes 2359300
  66.9 28.2 %all-to-all-start.1 = ((f32[32,24,128]{2,1,0:T(8,128)}), f32[32,24,128]{2,1,0:T(8,128)S(1)}, u32[]{:S(2)}, u32[]{:S(2)}) async-start(f32[32,24,128]{2,1,0:T(8,128)} %get-tuple-element.21), calls=%async_computation.1 | async-start | bytes 786432 | tf_op jit(solution)/shard_map/all_to_all | solution.py:478
  95.1 19.7 %copy-start = (f32[32,24,128]{2,1,0:T(8,128)}, f32[32,24,128]{2,1,0:T(8,128)S(1)}, u32[]{:S(2)}) copy-start(f32[32,24,128]{2,1,0:T(8,128)S(1)} %all-to-all-done.1.refs_0_) | copy-start | bytes 1179652

commit v4 on v3

--- a/solution.py
+++ b/solution.py
@@ -14,7 +14,7 @@
 BATCH = 128
 CHUNK = 256
 TEAM = 4
-WINDOW = 96
+WINDOW = 112
 LANES = 128
 AXES = ("row", "col")
 NT = (((1,), (1,)), ((), ()))

time: 119 us -> 120 us (level)
  starting transfers between devices: 15.6 us -> 19.1 us
  Pallas kernels: 60.9 us -> 58.3 us
    all_to_all x3, starting transfers between devices: 15.6 us -> 19.1 us  [exchange(): return lax.all_to_all(x, AXES, split_axis=0, concat_axis=0, tiled=True)]
    pallas_call x2, Pallas kernels: 48 us -> 45.5 us  [couple(): pl.pallas_call(functools.partial(couple_kernel, part), grid=(steps,), out...]
  transfers between devices with their start and end apart: 3 -> 3, of which waited for: 1 -> 1; matrix products, arithmetic and copies ran while one was open for 13% -> 13% of each run, Pallas kernels for 43% -> 41%
where the time goes in v4:
time: 120 us; the launch traced here: 119 us
  Pallas kernels  58.3 us (49%)
  starting transfers between devices  19.1 us (16%)
  blocking collectives  19 us (16%)
  matrix products  11.7 us (10%)
  waiting for transfers between devices  4.62 us (4%)
  local copies, waits for them, and re-layouts  2.69 us (2%)
  other arithmetic  2.45 us (2%)
    pallas_call x2, Pallas kernels, couple(): pl.pallas_call(functools.partial(couple_kernel, part), grid=(steps,), out...  45.5 us
    all_to_all x3, starting transfers between devices, exchange(): return lax.all_to_all(x, AXES, split_axis=0, concat_axis=0, tiled=True)  19.1 us
    all_to_all x1, blocking collectives, exchange(): return lax.all_to_all(x, AXES, split_axis=0, concat_axis=0, tiled=True)  19 us
    dot_general x1, matrix products, on_device(): jnp.einsum('cin,cnm->cim', node_disp, inverse, precision=highest)  11.7 us
    pallas_call x1, Pallas kernels, on_device(): pl.pallas_call(functools.partial(first_pack_kernel, local_count, pair_tot...  5.99 us
    all_to_all x3, waiting for transfers between devices, exchange(): return lax.all_to_all(x, AXES, split_axis=0, concat_axis=0, tiled=True)  4.62 us
    pallas_call x1, Pallas kernels, on_device(): pl.pallas_call(unpack_kernel, out_shape=jax.ShapeDtypeStruct((3, tile_tot...  3.59 us
    pallas_call x1, Pallas kernels, on_device(): pl.pallas_call(functools.partial(next_pack_kernel, part + 1), out_shape=j...  3.28 us
  transfers between devices with their start and end apart: 3, of which 1 were waited for; matrix products, arithmetic and copies ran while one was open for 13% of the time, Pallas kernels for 41%

profile of v4, /device:TPU:0, one launch (start us, length us, event | category | flops | bytes accessed | tf_op | source)
XLA Modules:
  0.0 118.7 jit_solution(3042283007236402595)
XLA Ops:
  0.6 0.8 copy.19
  1.4 0.7 reshape.57.ids
  2.0 6.0 %pack_0.1 = (f32[32,56,128]{2,1,0:T(8,128)}, f32[3,256,256]{2,1,0:T(8,128)}, s32[256]{0:T(256)}) custom-call(s32[256]{0:T(256)} %reshape.57.ids, f32[3,32,256]{2,1,0:T(8,128)} %bitcast.5, f32[3,32,256]{2,1,0:T(8,128)} %bitcast.7, s32[32,8,256]{2,1,0:T(8,128)} %refs_2_.1), custom_call_target="tpu_custom_call" | custom-call | tf_op jit(solution)/shard_map/pack_0/pallas_call | solution.py:491
  8.0 7.3 %all-to-all-start = ((f32[32,56,128]{2,1,0:T(8,128)}), f32[32,56,128]{2,1,0:T(8,128)S(1)}, u32[]{:S(2)}, u32[]{:S(2)}) async-start(f32[32,56,128]{2,1,0:T(8,128)} %get-tuple-element.16), calls=%async_computation | async-start | bytes 1835008 | tf_op jit(solution)/shard_map/all_to_all | solution.py:478
  15.4 1.0 fusion.15
  16.4 0.1 pad_maximum_fusion.2
  16.5 0.1 copy.20
  16.6 3.3 %pack_1.1 = f32[32,48,128]{2,1,0:T(8,128)} custom-call(s32[256]{0:T(256)} %get-tuple-element.14.pair_of, f32[3,32,256]{2,1,0:T(8,128)} %bitcast.6, f32[3,256,256]{2,1,0:T(8,128)} %get-tuple-element.15.loads), custom_call_target="tpu_custom_call" | custom-call | tf_op jit(solution)/shard_map/pack_1/pallas_call | solution.py:529
  19.9 1.0 multiply_reduce_fusion
  20.9 0.1 fusion.12
  21.0 0.1 fusion.4
  21.2 1.1 concatenate.17.refs_3_
  22.3 11.7 %reduce-precision_convert_fusion = (bf16[16,3,512]{2,1,0:T(4,128)(2,1)S(1)}, bf16[16,3,512]{2,1,0:T(4,128)(2,1)S(1)}) fusion(f32[16,512,512]{2,1,0:T(8,128)} %param.13, f32[16,3,512]{2,0,1:T(8,128)} %param.12), kind=kOutput, calls=%fused_computation.3 | convolution fusion | flops 151142400 | bytes 16973824 | tf_op jit(solution)/shard_map/cin,cnm->cim/dot_general | solution.py:505
  34.0 0.2 pad_maximum_fusion.refs_4_
  34.2 4.6 %all-to-all-done.refs_0_.refs_1_ = f32[32,56,128]{2,1,0:T(8,128)S(1)} async-done(((f32[32,56,128]{2,1,0:T(8,128)}), f32[32,56,128]{2,1,0:T(8,128)S(1)}, u32[]{:S(2)}, u32[]{:S(2)}) %all-to-all-start) | async-done | bytes 917536 | tf_op jit(solution)/shard_map/all_to_all | solution.py:478
  38.8 0.0 copy-start.1
  38.8 3.6 %all-to-all-start.2 = ((f32[32,48,128]{2,1,0:T(8,128)}), f32[32,48,128]{2,1,0:T(8,128)S(1)}, u32[]{:S(2)}, u32[]{:S(2)}) async-start(f32[32,48,128]{2,1,0:T(8,128)} %pack_1.1), calls=%async_computation.2 | async-start | bytes 1572864 | tf_op jit(solution)/shard_map/all_to_all | solution.py:478
  42.4 0.0 copy-done.1
  42.4 21.8 %couple_0.1 = (f32[32,24,128]{2,1,0:T(8,128)}, f32[16,8,512]{2,1,0:T(8,128)S(1)}) custom-call(f32[32,56,128]{2,1,0:T(8,128)} %copy-done.1, f32[32,56,128]{2,1,0:T(8,128)} %copy-done.1, bf16[128,128]{1,0:T(8,128)(2,1)S(1)} %pad.4.refs_2_, bf16[16,32,512]{2,1,0:T(8,128)(2,1)S(1)} %concatenate.17.refs_3_, bf16[16,16,512]{2,1,0:T(8,128)(2,1)S(1)} %pad_maximum_fusion.refs_4_), custom_call_target="tpu_custom_call" | custom-call | flops 335544320 | bytes 1376256 | tf_op jit(solution)/shard_map/couple_0/pallas_call | solution.py:433
  64.3 0.0 all-to-all-done.2.refs_1_
  64.3 0.0 copy-start.2
  64.3 8.2 %all-to-all-start.1 = ((f32[32,24,128]{2,1,0:T(8,128)}), f32[32,24,128]{2,1,0:T(8,128)S(1)}, u32[]{:S(2)}, u32[]{:S(2)}) async-start(f32[32,24,128]{2,1,0:T(8,128)} %get-tuple-element.21), calls=%async_computation.1 | async-start | bytes 786432 | tf_op jit(solution)/shard_map/all_to_all | solution.py:478
  72.5 0.0 copy-done.2
  72.5 23.6 %couple_1.1 = (f32[32,24,128]{2,1,0:T(8,128)S(1)}, f32[3,16,512]{2,1,0:T(8,128)}) custom-call(f32[32,56,128]{2,1,0:T(8,128)} %copy-done.1, f32[32,48,128]{2,1,0:T(8,128)} %copy-done.2, bf16[128,128]{1,0:T(8,128)(2,1)S(1)} %pad.4.refs_2_, bf16[16,32,512]{2,1,0:T(8,128)(2,1)S(1)} %concatenate.17.refs_3_, bf16[16,16,512]{2,1,0:T(8,128)(2,1)S(1)} %pad_maximum_fusion.refs_4_, ...), custom_call_target="tpu_custom_call" | custom-call | flops 335544320 | bytes 1179648 | tf_op jit(solution)/shard_map/couple_1/pallas_call | solution.py:433
  96.1 0.0 all-to-all-done.1.refs_0_
  96.1 0.0 copy-start
  96.1 19.0 %all_to_all.20.refs_1_ = f32[32,24,128]{2,1,0:T(8,128)} all-to-all(f32[32,24,128]{2,1,0:T(8,128)S(1)} %get-tuple-element.24), channel_id=1, replica_groups=mesh['row'=4,'col'=8] {'row','col'}, dimensions={0} | all-to-all | bytes 786432 | tf_op jit(solution)/shard_map/all_to_all | solution.py:478
  115.1 0.0 copy-done
  115.1 3.6 %unpack.1 = f32[3,32,256]{2,1,0:T(8,128)} custom-call(s32[256]{0:T(256)} %get-tuple-element.14.pair_of, f32[32,24,128]{2,1,0:T(8,128)} %copy-done, f32[32,24,128]{2,1,0:T(8,128)} %all_to_all.20.refs_1_, s32[32,8,256]{2,1,0:T(8,128)} %refs_2_.1), custom_call_target="tpu_custom_call" | custom-call | tf_op jit(solution)/shard_map/unpack/pallas_call | solution.py:546
  (6 shorter events, 0.1 us)
Async XLA Ops:
  8.0 30.7 %all-to-all-start = ((f32[32,56,128]{2,1,0:T(8,128)}), f32[32,56,128]{2,1,0:T(8,128)S(1)}, u32[]{:S(2)}, u32[]{:S(2)}) async-start(f32[32,56,128]{2,1,0:T(8,128)} %get-tuple-element.16), calls=%async_computation | async-start | bytes 1835008 | tf_op jit(solution)/shard_map/all_to_all | solution.py:478
  38.8 3.6 %copy-start.1 = (f32[32,56,128]{2,1,0:T(8,128)}, f32[32,56,128]{2,1,0:T(8,128)S(1)}, u32[]{:S(2)}) copy-start(f32[32,56,128]{2,1,0:T(8,128)S(1)} %all-to-all-done.refs_0_.refs_1_) | copy-start | bytes 2752516
  38.8 25.5 %all-to-all-start.2 = ((f32[32,48,128]{2,1,0:T(8,128)}), f32[32,48,128]{2,1,0:T(8,128)S(1)}, u32[]{:S(2)}, u32[]{:S(2)}) async-start(f32[32,48,128]{2,1,0:T(8,128)} %pack_1.1), calls=%async_computation.2 | async-start | bytes 1572864 | tf_op jit(solution)/shard_map/all_to_all | solution.py:478
  64.3 8.2 %copy-start.2 = (f32[32,48,128]{2,1,0:T(8,128)}, f32[32,48,128]{2,1,0:T(8,128)S(1)}, u32[]{:S(2)}) copy-start(f32[32,48,128]{2,1,0:T(8,128)S(1)} %all-to-all-done.2.refs_1_) | copy-start | bytes 2359300
  64.3 31.8 %all-to-all-start.1 = ((f32[32,24,128]{2,1,0:T(8,128)}), f32[32,24,128]{2,1,0:T(8,128)S(1)}, u32[]{:S(2)}, u32[]{:S(2)}) async-start(f32[32,24,128]{2,1,0:T(8,128)} %get-tuple-element.21), calls=%async_computation.1 | async-start | bytes 786432 | tf_op jit(solution)/shard_map/all_to_all | solution.py:478
  96.1 19.0 %copy-start = (f32[32,24,128]{2,1,0:T(8,128)}, f32[32,24,128]{2,1,0:T(8,128)S(1)}, u32[]{:S(2)}) copy-start(f32[32,24,128]{2,1,0:T(8,128)S(1)} %all-to-all-done.1.refs_0_) | copy-start | bytes 1179652
